TPU v7x, 32 devices: a whole 2x2x4 slice. The times are simulated.
32 devices in a mesh: gx: 4 (over z), gy: 8 (over y, x, core).
Axes of the slice: x: 2, y: 2, z: 4, core: 2. Of those that a mesh axis runs over, the one named last changes fastest.
Arguments:
- policy_logp: float32 [16, 512, 4096], P('gy', 'gx'), may hold values from -2 to 0
- anchor_logp: float32 [16, 512, 4096], P('gy', 'gx'), may hold values from -2 to 0
- lengths: int32 [16, 512], P('gy', 'gx'), may hold values from 512 to 4096
- rewards: int32 [16, 512], P('gy', 'gx'), may hold values from 0 to 8
- slot_prompt: int32 [16, 512], P('gy', 'gx'), may hold values from 0 to 511, as said below
Outputs:
- token_grad: float32 [16, 512, 4096], P(None, ('gx', 'gy'))
- sample_loss: float32 [16, 512], P(None, ('gx', 'gy'))
- advantage: float32 [16, 512], P(None, ('gx', 'gy'))
Inputs may be any that keep to these rules, and one draw needn't show every extreme that they name: `slot_prompt`: for every member k and every aligned block of 128 slots, the slots of the block hold each prompt of the same block exactly once.
All inputs are finite; a program needn't handle non-finite values.
Results may differ from a plain program's by a relative error of at most 0.00002.
Values sent between devices are 32-bit elements; how exact they have to be, the bound alone decides.
A program may use at most 64 MiB of HBM per device.

v0:
```python
import functools

import jax
import jax.numpy as jnp
from jax import lax
from jax.experimental import pallas as pl
from jax.experimental.pallas import tpu as pltpu
from jax.sharding import PartitionSpec as P

kl_weight = 0.1
LANES = 128
CHUNKS = 8
MESH = pl.DeviceIdType.MESH
ROLES = 4
STRIPS = 16
SHIFTS = 5
HEAD_BLOCKS = 4
STRIP_BLOCKS = 75
FIRST_ORDER = (2, 4, 3, 5, 6, 7)


def partner(index, off, count):
    out, bit = index, 1
    while bit < count:
        if off & bit:
            out = out + bit - 2 * bit * lax.rem(index // bit, 2)
        bit *= 2
    return out


def offsets_by_distance(count):
    far = max(bin(off // 2).count("1") for off in range(1, count))
    near = [off for off in range(1, count) if bin(off // 2).count("1") < far]
    return near, [off for off in range(1, count) if off not in near]


def permuted(onehot, rows):
    high = rows.astype(jnp.bfloat16)
    rest = rows - high.astype(jnp.float32)
    middle = rest.astype(jnp.bfloat16)
    low = (rest - middle.astype(jnp.float32)).astype(jnp.bfloat16)
    dot = functools.partial(jnp.dot, preferred_element_type=jnp.float32)
    return dot(onehot, high) + dot(onehot, middle) + dot(onehot, low)


def folded(x):
    out = x[:, :LANES]
    for start in range(LANES, x.shape[1], LANES):
        out = out + x[:, start : start + LANES]
    return out


def exchange(
    n_gx, n_gy, policy_hbm, anchor_hbm, len_ref, reward_ref, prompt_ref,
    raw_hbm, heads_ref, tails_ref, ntok_ref,
    policy, anchor, sendbuf, onehot, len_col, sum_policy, sum_kl,
    heads_send, heads_recv, tails_send, tails_recv, counts,
    load_sem, send_sem, recv_sem, own_sem,
    head_send_sem, head_recv_sem, tail_send_sem, tail_recv_sem, count_send_sem, count_recv_sem,
):
    gx, gy = lax.axis_index("gx"), lax.axis_index("gy")
    members_dev, slots, seq = policy_hbm.shape
    part = slots // n_gy
    width = seq // CHUNKS

    near, far = offsets_by_distance(n_gy)
    barrier = pltpu.get_barrier_semaphore()
    for off in range(1, n_gy):
        pl.semaphore_signal(barrier, inc=1, device_id=(gx, partner(gy, off, n_gy)), device_id_type=MESH)
    for off in range(1, n_gx):
        pl.semaphore_signal(barrier, inc=1, device_id=(lax.rem(gx + off, n_gx), gy), device_id_type=MESH)

    def loads(c):
        cols = pl.ds(pl.multiple_of(c * width, LANES), width)
        return (
            pltpu.make_async_copy(policy_hbm.at[:, :, cols], policy.at[c], load_sem.at[0, c]),
            pltpu.make_async_copy(anchor_hbm.at[:, :, cols], anchor.at[c], load_sem.at[1, c]),
        )

    for c in range(CHUNKS):
        for copy in loads(c):
            copy.start()

    sublane = lax.broadcasted_iota(jnp.int32, (slots, slots), 0)
    lane = lax.broadcasted_iota(jnp.int32, (slots, slots), 1)
    column = lax.broadcasted_iota(jnp.int32, (slots, LANES), 1)
    local_tokens = jnp.sum(len_ref[...].astype(jnp.float32))
    for m in range(members_dev):
        seq_len = len_ref[m : m + 1, :].astype(jnp.float32)
        reward = reward_ref[m : m + 1, :].astype(jnp.float32) * 0.25
        match = sublane == lax.rem(prompt_ref[m : m + 1, :], slots)
        onehot[m] = jnp.where(match, 1.0, 0.0).astype(jnp.bfloat16)
        len_col[m] = jnp.broadcast_to(
            jnp.sum(jnp.where(sublane == lane, seq_len, 0.0), axis=1, keepdims=True), (slots, LANES)
        )
        sorted_len = jnp.sum(jnp.where(match, seq_len, 0.0), axis=1, keepdims=True)
        sorted_reward = jnp.sum(jnp.where(match, reward, 0.0), axis=1, keepdims=True)
        heads_send[m] = jnp.where(
            column == 0, sorted_len, jnp.where(column == 1, sorted_reward, local_tokens)
        )
    sum_policy[...] = jnp.zeros_like(sum_policy)
    sum_kl[...] = jnp.zeros_like(sum_kl)

    def compute(c):
        for copy in loads(c):
            copy.wait()
        positions = (lax.broadcasted_iota(jnp.int32, (slots, width), 1) + c * width).astype(jnp.float32)
        for m in range(members_dev):
            pol = policy[c, m]
            log_ratio = anchor[c, m] - pol
            ratio = jnp.exp(log_ratio)
            valid = positions < len_col[m][:, :1]
            sum_policy[m] += folded(jnp.where(valid, pol, 0.0))
            sum_kl[m] += folded(jnp.where(valid, kl_weight * (ratio - log_ratio - 1.0), 0.0))
            sendbuf[c, m] = permuted(onehot[m], kl_weight * (1.0 - ratio))

    def rows_of(device):
        return pl.ds(pl.multiple_of(device * part, part), part)

    my_members = pl.ds(gy * members_dev, members_dev)

    def sends(c, offs):
        cols = pl.ds(pl.multiple_of(c * width, LANES), width)
        copies = []
        for off in offs:
            peer = partner(gy, off, n_gy)
            copies.append(
                pltpu.make_async_remote_copy(
                    src_ref=sendbuf.at[c, :, rows_of(peer), :],
                    dst_ref=raw_hbm.at[my_members, :, cols],
                    send_sem=send_sem.at[off - 1],
                    recv_sem=recv_sem.at[off - 1],
                    device_id=(gx, peer),
                    device_id_type=MESH,
                )
            )
        return copies

    def own(c):
        cols = pl.ds(pl.multiple_of(c * width, LANES), width)
        return pltpu.make_async_copy(
            sendbuf.at[c, :, rows_of(gy), :], raw_hbm.at[my_members, :, cols], own_sem.at[c]
        )

    def small_sends(src, dst, send, recv):
        copies = []
        for off in range(1, n_gy):
            peer = partner(gy, off, n_gy)
            copies.append(
                pltpu.make_async_remote_copy(
                    src_ref=src.at[:, rows_of(peer), :],
                    dst_ref=dst.at[my_members],
                    send_sem=send.at[off - 1],
                    recv_sem=recv.at[off - 1],
                    device_id=(gx, peer),
                    device_id_type=MESH,
                )
            )
        copies.append(pltpu.make_async_copy(src.at[:, rows_of(gy), :], dst.at[my_members], send.at[n_gy - 1]))
        return copies

    def count_sends():
        return [
            pltpu.make_async_remote_copy(
                src_ref=counts.at[0],
                dst_ref=counts.at[off],
                send_sem=count_send_sem.at[off - 1],
                recv_sem=count_recv_sem.at[off - 1],
                device_id=(lax.rem(gx + off, n_gx), gy),
                device_id_type=MESH,
            )
            for off in range(1, n_gx)
        ]

    compute(0)
    pl.semaphore_wait(barrier, n_gy - 1 + n_gx - 1)
    head_copies = small_sends(heads_send, heads_recv, head_send_sem, head_recv_sem)
    for copy in head_copies:
        copy.start()

    def step(c, carry):
        for copy in sends(c - 1, near):
            copy.start()
        own(c - 1).start()
        compute(c)
        return carry

    lax.fori_loop(1, CHUNKS, step, 0)
    for copy in sends(CHUNKS - 1, near):
        copy.start()

    def far_step(c, carry):
        for copy in sends(c, far):
            copy.start()
        return carry

    lax.fori_loop(0, CHUNKS, far_step, 0)
    own(CHUNKS - 1).start()

    for m in range(members_dev):
        s1 = jnp.sum(permuted(onehot[m], sum_policy[m]), axis=1, keepdims=True)
        s2 = jnp.sum(permuted(onehot[m], sum_kl[m]), axis=1, keepdims=True)
        tails_send[m] = jnp.where(column == 0, s1, s2)
    for copy in head_copies:
        copy.wait()
    tokens = jnp.zeros((8, LANES), jnp.float32)
    for source in range(n_gy):
        tokens = tokens + heads_recv[source * members_dev, :8, :]
    counts[0] = tokens
    heads_ref[...] = heads_recv[...]
    tail_copies = small_sends(tails_send, tails_recv, tail_send_sem, tail_recv_sem)
    for copy in tail_copies:
        copy.start()
    count_copies = count_sends()
    for copy in count_copies:
        copy.start()
    for copy in count_copies:
        copy.wait()
    ntok_ref[...] = jnp.sum(counts[...], axis=0)
    for copy in tail_copies:
        copy.wait()
    tails_ref[...] = tails_recv[...]
    for c in range(CHUNKS):
        own(c).wait()
    for off in range(1, n_gy):
        source = partner(gy, off, n_gy)
        landed = raw_hbm.at[pl.ds(source * members_dev, members_dev)]
        pltpu.make_async_copy(landed, landed, recv_sem.at[off - 1]).wait()
        pltpu.make_async_copy(landed, landed, send_sem.at[off - 1]).wait()


def finish(samples, raw, heads, tails, ntok, grad, loss, adv, done, done_sem):
    members, part, seq = raw.shape
    tokens = ntok[:1, 2:3]
    total = jnp.sum(heads[...], axis=0)
    advantage = (members * heads[:, :, 1:2] - total[None, :, 1:2]) / (members - 1)
    positions = lax.broadcasted_iota(jnp.int32, (part, seq), 1).astype(jnp.float32)
    scale = samples * seq / tokens

    def store(k):
        return pltpu.make_async_copy(done.at[k], grad.at[k], done_sem.at[k])

    for k in range(members):
        done[k] = jnp.where(positions < heads[k, :, :1], raw[k] - advantage[k], 0.0) * scale
        if k > 0:
            store(k - 1).start()
    shape = (members, part, LANES)
    eye = lax.broadcasted_iota(jnp.int32, shape, 1) == lax.broadcasted_iota(jnp.int32, shape, 2)
    store(members - 1).start()
    value = (tails[:, :, 1:2] - advantage * tails[:, :, :1]) * (samples / tokens)[None]
    loss[...] = jnp.sum(jnp.where(eye, value, 0.0), axis=1)[:, :part]
    adv[...] = jnp.sum(jnp.where(eye, advantage, 0.0), axis=1)[:, :part]
    for k in range(members):
        store(k).wait()


def unpacked_body(n_gx, n_gy, policy_logp, anchor_logp, lengths, rewards, slot_prompt):
    members_dev, slots, seq = policy_logp.shape
    members, part = members_dev * n_gy, slots // n_gy
    f32 = jnp.float32
    chunked = (CHUNKS, members_dev, slots, seq // CHUNKS)
    small = (members, part, LANES)
    hbm_spec = pl.BlockSpec(memory_space=pltpu.HBM)
    vmem_spec = pl.BlockSpec(memory_space=pltpu.VMEM)
    dma = pltpu.SemaphoreType.DMA
    raw, heads, tails, ntok = pl.pallas_call(
        functools.partial(exchange, n_gx, n_gy),
        out_shape=(
            pltpu.VMEM((members, part, seq), f32),
            pltpu.VMEM(small, f32),
            pltpu.VMEM(small, f32),
            pltpu.VMEM((8, LANES), f32),
        ),
        in_specs=[hbm_spec, hbm_spec, vmem_spec, vmem_spec, vmem_spec],
        out_specs=(vmem_spec, vmem_spec, vmem_spec, vmem_spec),
        scratch_shapes=[
            pltpu.VMEM(chunked, f32),
            pltpu.VMEM(chunked, f32),
            pltpu.VMEM(chunked, f32),
            pltpu.VMEM((members_dev, slots, slots), jnp.bfloat16),
            pltpu.VMEM((members_dev, slots, LANES), f32),
            pltpu.VMEM((members_dev, slots, LANES), f32),
            pltpu.VMEM((members_dev, slots, LANES), f32),
            pltpu.VMEM((members_dev, slots, LANES), f32),
            pltpu.VMEM(small, f32),
            pltpu.VMEM((members_dev, slots, LANES), f32),
            pltpu.VMEM(small, f32),
            pltpu.VMEM((n_gx, 8, LANES), f32),
            dma((2, CHUNKS)),
            dma((n_gy - 1,)),
            dma((n_gy - 1,)),
            dma((CHUNKS,)),
            dma((n_gy,)),
            dma((n_gy - 1,)),
            dma((n_gy,)),
            dma((n_gy - 1,)),
            dma((n_gx - 1,)),
            dma((n_gx - 1,)),
        ],
        compiler_params=pltpu.CompilerParams(collective_id=1, has_side_effects=True, vmem_limit_bytes=56 * 2**20),
    )(policy_logp, anchor_logp, lengths, rewards, slot_prompt)
    samples = members * slots * n_gx
    return pl.pallas_call(
        functools.partial(finish, samples),
        out_shape=(
            jax.ShapeDtypeStruct((members, part, seq), f32),
            jax.ShapeDtypeStruct((members, part), f32),
            jax.ShapeDtypeStruct((members, part), f32),
        ),
        in_specs=[vmem_spec] * 4,
        out_specs=(hbm_spec, vmem_spec, vmem_spec),
        scratch_shapes=[pltpu.VMEM((members, part, seq), f32), dma((members,))],
        compiler_params=pltpu.CompilerParams(vmem_limit_bytes=32 * 2**20),
    )(raw, heads, tails, ntok)


def row_of(column):
    n = column.shape[0]
    eye = lax.broadcasted_iota(jnp.int32, (n, n), 0) == lax.broadcasted_iota(jnp.int32, (n, n), 1)
    return jnp.sum(jnp.where(eye, column, 0.0), axis=0, keepdims=True)


def row_sums(place, targets, values):
    out = None
    for target, value in zip(targets, values):
        here = jnp.sum(jnp.where(place == target, value, 0.0), axis=1, keepdims=True)
        out = here if out is None else out + here
    return out


def strip_spot(rank):
    first, second, third = rank < STRIPS, rank < 2 * STRIPS, rank < 3 * STRIPS
    strip = jnp.where(
        first, rank, jnp.where(second, 2 * STRIPS - 1 - rank, jnp.where(third, rank - 2 * STRIPS, 4 * STRIPS - 1 - rank))
    )
    return jnp.where(first, 0.0, jnp.where(second, 3.0, jnp.where(third, 2.0, 1.0))) * STRIPS + strip


def strip_plan(len_row, len_column, group_row, group_column, index_row, index_column, n_groups, seq):
    rows = ROLES * STRIPS
    key_row = group_row * ((seq + 1) * rows) + len_row * rows + index_row
    key_column = group_column * ((seq + 1) * rows) + len_column * rows + index_column
    above_row = jnp.sum(jnp.where(key_column > key_row, 1.0, 0.0), axis=0, keepdims=True)
    above_column = jnp.sum(jnp.where(key_row > key_column, 1.0, 0.0), axis=1, keepdims=True)
    return (
        strip_spot(above_row - rows * (n_groups - 1 - group_row)),
        strip_spot(above_column - rows * (n_groups - 1 - group_column)),
    )


def tail_blocks(lens):
    return jnp.floor((lens + (LANES - 1)) * (1.0 / LANES)) - HEAD_BLOCKS


def shift_bits(count):
    shift = count.astype(jnp.int32)
    return [(lax.shift_right_logical(shift, k) & 1) == 1 for k in range(SHIFTS)]


def shifted_up(blocks, bits, reach):
    for k in range(SHIFTS):
        step, n = 2**k, len(blocks)
        moved = []
        for p in range(min(n + step, reach)):
            if p < step:
                moved.append(blocks[p])
            elif p >= n:
                moved.append(blocks[p - step])
            else:
                moved.append(jnp.where(bits[k], blocks[p - step], blocks[p]))
        blocks = moved
    return blocks


def shifted_down(blocks, bits, count):
    for k in reversed(range(SHIFTS)):
        step = 2**k
        keep = min(len(blocks), count + step - 1)
        blocks = [
            jnp.where(bits[k], blocks[p + step], blocks[p]) if p + step < len(blocks) else blocks[p] for p in range(keep)
        ]
    return blocks


def peer_of(index, off, count):
    out, bit = 0, 1
    while bit < count:
        a, b = lax.rem(index // bit, 2), lax.rem(off // bit, 2)
        out = out + bit * (a + b - 2 * a * b)
        bit *= 2
    return out


def packed_exchange(
    n_gx, n_gy, policy_hbm, anchor_hbm, len_hbm, reward_hbm, prompt_hbm,
    done, loss_ref, adv_ref, over_ref,
    policy, anchor, len_ref, reward_ref, prompt_ref, onehot, ordered, got, heads_in, sendbuf, recvbuf, roles,
    deal, undeal, cnt, rcnt, len_col, sum_policy, sum_kl, len_rows, adv_rows,
    info_send, info_got, info_recv, tails_send, tails_recv, counts, needs,
    small_sem, load_sem, give_send_sem, give_recv_sem, first_send_sem, first_recv_sem, strip_send_sem, strip_recv_sem,
    info_send_sem, info_recv_sem, tail_send_sem, tail_recv_sem, count_send_sem, count_recv_sem, need_send_sem, need_recv_sem,
):
    gx, gy = lax.axis_index("gx"), lax.axis_index("gy")
    core, chip = lax.rem(gy, 2), gy // 2
    mate = chip * 2 + 1 - core
    members_dev, slots, seq = policy_hbm.shape
    members, part = members_dev * n_gy, slots // n_gy
    chips = n_gy // 2
    width = seq // CHUNKS
    nblocks = seq // LANES - HEAD_BLOCKS
    rows = members_dev * part
    pool = 2 * rows
    total_rows = chips * pool
    samples = members * slots * n_gx
    info_lane, fill_lane = 16, 17
    f32 = jnp.float32

    small_loads = [
        pltpu.make_async_copy(src, dst, small_sem.at[k])
        for k, (src, dst) in enumerate(((len_hbm, len_ref), (prompt_hbm, prompt_ref), (reward_hbm, reward_ref)))
    ]
    for copy in small_loads:
        copy.start()

    def loads(c):
        cols = pl.ds(pl.multiple_of(c * width, LANES), width)
        return (
            pltpu.make_async_copy(policy_hbm.at[:, :, cols], policy.at[c], load_sem.at[0, c]),
            pltpu.make_async_copy(anchor_hbm.at[:, :, cols], anchor.at[c], load_sem.at[1, c]),
        )

    for copy in loads(0):
        copy.start()
    barrier = pltpu.get_barrier_semaphore()
    for off in range(1, n_gy):
        pl.semaphore_signal(barrier, inc=1, device_id=(gx, partner(gy, off, n_gy)), device_id_type=MESH)
    for off in range(1, n_gx):
        pl.semaphore_signal(barrier, inc=1, device_id=(lax.rem(gx + off, n_gx), gy), device_id_type=MESH)
    for c in range(1, CHUNKS):
        for copy in loads(c):
            copy.start()
    for copy in small_loads:
        copy.wait()

    lens = [len_ref[m : m + 1, :].astype(f32) for m in range(members_dev)]
    targets = []
    for m in range(members_dev):
        spot = lax.rem(prompt_ref[m : m + 1, :], slots)
        device = spot // part
        other = lax.rem(device + core, 2)
        target = (other * chips + device // 2) * rows + m * part + spot - device * part
        targets.append(target.astype(f32))
    place = lax.broadcasted_iota(jnp.int32, (total_rows, slots), 0).astype(f32)
    for m in range(members_dev):
        onehot[:, m * slots : (m + 1) * slots] = jnp.where(place == targets[m], 1.0, 0.0).astype(jnp.bfloat16)

    def put_in_order(c):
        for copy in loads(c):
            copy.wait()
        values = kl_weight * (1.0 - jnp.exp(anchor[c] - policy[c]))
        out = permuted(onehot[...], values.reshape(members_dev * slots, width))
        cols = pl.ds(pl.multiple_of(c * width, LANES), width)
        ordered[:, :, :, cols] = out.reshape(2, chips, rows, width)

    def give(c):
        cols = pl.ds(pl.multiple_of(c * width, LANES), width)
        return pltpu.make_async_remote_copy(
            src_ref=ordered.at[1, :, :, cols],
            dst_ref=got.at[:, :, cols],
            send_sem=give_send_sem,
            recv_sem=give_recv_sem,
            device_id=(gx, mate),
            device_id_type=MESH,
        )

    def first_send(off):
        peer = partner(gy, off, n_gy)
        return pltpu.make_async_remote_copy(
            src_ref=ordered.at[off % 2, peer // 2, :, pl.ds(0, width)],
            dst_ref=heads_in.at[gy],
            send_sem=first_send_sem.at[off - 2],
            recv_sem=first_recv_sem.at[off - 2],
            device_id=(gx, peer),
            device_id_type=MESH,
        )

    put_in_order(0)
    pl.semaphore_wait(barrier, n_gy - 1 + n_gx - 1)
    first_copies = [first_send(off) for off in FIRST_ORDER]
    for copy in first_copies:
        copy.start()
    give(0).start()

    tile_lane = lax.broadcasted_iota(jnp.int32, (n_gy, 8, LANES), 2)
    groups = rows // 8
    local_tokens = sum(jnp.sum(length) for length in lens)

    def tiles(columns, base):
        out = base
        for f, column in enumerate(columns):
            split = column.reshape(n_gy, groups, 8, 1)
            for g in range(groups):
                out = jnp.where(tile_lane == g * 4 + f, split[:, g], out)
        return out

    def column_in(tile, f):
        parts = [tile[:, :, g * 4 + f : g * 4 + f + 1][:, None] for g in range(groups)]
        return jnp.concatenate(parts, axis=1)

    own_len = row_sums(place, targets, lens)
    rewards = [reward_ref[m : m + 1, :].astype(f32) * 0.25 for m in range(members_dev)]
    own_reward = row_sums(place, targets, rewards)
    info_send[...] = tiles((own_len, own_reward), jnp.broadcast_to(local_tokens, (n_gy, 8, LANES)))

    def tile_sends(src, dst, send, recv, offs):
        copies = []
        for off in offs:
            peer = partner(gy, off, n_gy)
            copies.append(
                pltpu.make_async_remote_copy(
                    src_ref=src.at[off % 2 * chips + peer // 2],
                    dst_ref=dst.at[gy],
                    send_sem=send.at[off - 1],
                    recv_sem=recv.at[off - 1],
                    device_id=(gx, peer),
                    device_id_type=MESH,
                )
            )
        return copies

    mate_info = pltpu.make_async_remote_copy(
        src_ref=info_send.at[pl.ds(chips, chips)],
        dst_ref=info_got,
        send_sem=info_send_sem.at[0],
        recv_sem=info_recv_sem.at[0],
        device_id=(gx, mate),
        device_id_type=MESH,
    )
    info_copies = [mate_info] + tile_sends(info_send, info_recv, info_send_sem, info_recv_sem, range(2, n_gy))
    for copy in info_copies:
        copy.start()

    def order_step(c, carry):
        put_in_order(c)
        give(c).start()
        return carry

    lax.fori_loop(1, CHUNKS, order_step, 0)

    mate_info.wait()
    pair_lens = jnp.concatenate(
        [own_len[: chips * rows].reshape(chips, 1, rows, 1), column_in(info_got[...], 0).reshape(chips, 1, rows, 1)], axis=1
    ).reshape(total_rows, 1)
    row = lax.broadcasted_iota(jnp.int32, (1, total_rows), 1)
    column = lax.broadcasted_iota(jnp.int32, (total_rows, 1), 0)

    def pair_index(i):
        inside = lax.rem(i, pool)
        return (lax.rem(inside // rows + core, 2) * rows + lax.rem(inside, rows)).astype(f32)

    pair_row = row_of(pair_lens)
    spot_row, _ = strip_plan(
        pair_row, pair_lens, (row // pool).astype(f32), (column // pool).astype(f32), pair_index(row), pair_index(column),
        chips, seq,
    )
    wide = lax.broadcasted_iota(jnp.int32, (total_rows, total_rows), 0).astype(f32)

    def strip_counts(spots, lens_row):
        return row_sums(wide, [spots + (row // pool).astype(f32) * pool], [tail_blocks(lens_row)])

    pair_counts = strip_counts(spot_row, pair_row)
    cnt[...] = jnp.broadcast_to(pair_counts, cnt.shape)
    fill = jnp.sum(pair_counts.reshape(chips, ROLES, STRIPS, 1), axis=1)
    sent_chip = lax.broadcasted_iota(jnp.int32, (chips, STRIPS, 1), 0) != chip
    local_fill = jnp.max(jnp.where(sent_chip, fill, 0.0))
    square = lax.broadcasted_iota(jnp.int32, (pool, pool), 0).astype(f32)
    for s in range(chips):
        deal[s] = jnp.where(square == spot_row[:, s * pool : (s + 1) * pool], 1.0, 0.0).astype(jnp.bfloat16)
    pltpu.make_async_copy(got, got, give_recv_sem).wait()

    def strip_send(t, there):
        return pltpu.make_async_remote_copy(
            src_ref=sendbuf.at[there],
            dst_ref=recvbuf.at[chip],
            send_sem=strip_send_sem.at[t],
            recv_sem=strip_recv_sem.at[t],
            device_id=(gx, there * 2 + core),
            device_id_type=MESH,
        )

    reach = 2 * nblocks

    def pack(there):
        for c in range(1, CHUNKS):
            both = jnp.concatenate(
                [ordered[0, there, :, c * width : (c + 1) * width], got[there, :, c * width : (c + 1) * width]], axis=0
            )
            roles[:, (c - 1) * width : c * width] = permuted(deal[there], both)
        for half in range(STRIPS // 8):

            def count(role):
                at = there * pool + role * STRIPS + half * 8
                return cnt[pl.ds(pl.multiple_of(at, 8), 8), :]

            def blocks(role):
                at = role * STRIPS + half * 8
                return [roles[at : at + 8, j * LANES : (j + 1) * LANES] for j in range(nblocks)]

            def side(outer, inner):
                n = count(outer)
                behind = shifted_up(blocks(inner), shift_bits(n), reach)
                near_end = blocks(outer)
                return [jnp.where(n > p, near_end[p], behind[p]) for p in range(nblocks)] + behind[nblocks:]

            left, right = side(0, 1), side(3, 2)
            left_n = count(0) + count(1)
            for p in range(STRIP_BLOCKS):
                q = STRIP_BLOCKS - 1 - p
                if q >= reach:
                    value = left[p]
                elif p >= reach:
                    value = right[q]
                else:
                    value = jnp.where(left_n > p, left[p], right[q])
                sendbuf[there, half * 8 : half * 8 + 8, p * LANES : (p + 1) * LANES] = value

    def near_step(t, carry):
        there = peer_of(chip, t + 1, chips)
        pack(there)
        strip_send(t, there).start()
        return carry

    lax.fori_loop(0, 2, near_step, 0)

    info_recv[gy] = info_send[chip]
    for copy in info_copies[1:]:
        copy.wait()
    info_recv[mate] = info_got[chip]
    arrived = info_recv[...]
    counts[0] = jnp.sum(arrived, axis=0)

    def axis_sends(buf, send, recv):
        return [
            pltpu.make_async_remote_copy(
                src_ref=buf.at[0],
                dst_ref=buf.at[off],
                send_sem=send.at[off - 1],
                recv_sem=recv.at[off - 1],
                device_id=(lax.rem(gx + off, n_gx), gy),
                device_id_type=MESH,
            )
            for off in range(1, n_gx)
        ]

    count_copies = axis_sends(counts, count_send_sem, count_recv_sem)
    for copy in count_copies:
        copy.start()

    eye = lax.broadcasted_iota(jnp.int32, (slots, slots), 0) == lax.broadcasted_iota(jnp.int32, (slots, slots), 1)
    for m in range(members_dev):
        len_col[m] = jnp.broadcast_to(jnp.sum(jnp.where(eye, lens[m], 0.0), axis=1, keepdims=True), (slots, LANES))
    sum_policy[...] = jnp.zeros_like(sum_policy)
    sum_kl[...] = jnp.zeros_like(sum_kl)

    def sum_step(c, carry):
        positions = (lax.broadcasted_iota(jnp.int32, (slots, width), 1) + c * width).astype(f32)
        for m in range(members_dev):
            pol = policy[c, m]
            log_ratio = anchor[c, m] - pol
            ratio = jnp.exp(log_ratio)
            valid = positions < len_col[m][:, :1]
            sum_policy[m] += folded(jnp.where(valid, pol, 0.0))
            sum_kl[m] += folded(jnp.where(valid, kl_weight * (ratio - log_ratio - 1.0), 0.0))
        return carry

    lax.fori_loop(0, CHUNKS, sum_step, 0)
    sums = []
    for buf in (sum_policy, sum_kl):
        per_member = [row_of(jnp.sum(buf[m], axis=1, keepdims=True)) for m in range(members_dev)]
        sums.append(row_sums(place, targets, per_member))
    tails_send[...] = tiles(sums, jnp.broadcast_to(local_fill, (n_gy, 8, LANES)))
    tail_copies = tile_sends(tails_send, tails_recv, tail_send_sem, tail_recv_sem, range(1, n_gy))
    for copy in tail_copies:
        copy.start()
    tails_recv[gy] = tails_send[chip]

    far = peer_of(chip, chips - 1, chips)
    pack(far)
    strip_send(chips - 2, far).start()

    for copy in count_copies:
        copy.wait()
    tokens = counts[0]
    for off in range(1, n_gx):
        tokens = tokens + counts[off]
    ntok = tokens[:1, info_lane : info_lane + 1]
    scale = samples * seq / ntok
    got_len = column_in(arrived, 0).reshape(total_rows, 1)
    got_row = row_of(got_len)
    reward = column_in(arrived, 1).reshape(members, part, 1)
    advantage = (members * reward - jnp.sum(reward, axis=0)[None]) / (members - 1)
    adv_rows[...] = jnp.broadcast_to(advantage, adv_rows.shape)
    len_rows[...] = jnp.broadcast_to(got_len.reshape(members, part, 1), len_rows.shape)
    got_spot_row, got_spot = strip_plan(
        got_row, got_len, (row // pool).astype(f32), (column // pool).astype(f32),
        lax.rem(row, pool).astype(f32), lax.rem(column, pool).astype(f32), chips, seq,
    )
    rcnt[...] = jnp.broadcast_to(strip_counts(got_spot_row, got_row), rcnt.shape)
    pick = got_spot == lax.broadcasted_iota(jnp.int32, (total_rows, LANES), 1).astype(f32)
    undeal[...] = jnp.where(pick, 1.0, 0.0).astype(jnp.bfloat16).reshape(chips, pool, LANES)
    lane_width = lax.broadcasted_iota(jnp.int32, (part, width), 1).astype(f32)

    def finish_rows(k, start, value):
        value = (value - adv_rows[k][:, :1]) * scale
        valid = lane_width < len_rows[k][:, :1] - start
        done[k, :, start : start + width] = jnp.where(valid, value, 0.0)

    def own_step(which, source):
        for m in range(members_dev):
            for c in range(CHUNKS):
                finish_rows(source * members_dev + m, c * width, which(m * part, c * width))

    own_step(lambda r, s: ordered[0, chip, r : r + part, s : s + width], gy)
    own_step(lambda r, s: got[chip, r : r + part, s : s + width], mate)

    def first_wait(off):
        landed = heads_in.at[0]
        pltpu.make_async_copy(landed, landed, first_recv_sem.at[off - 2]).wait()

    def first_step(off, carry):
        first_wait(off)
        source = peer_of(gy, off, n_gy)
        for m in range(members_dev):
            finish_rows(source * members_dev + m, 0, heads_in[source, m * part : (m + 1) * part, :])
        return carry

    lax.fori_loop(2, n_gy, first_step, 0)

    def unpack(t):
        there = peer_of(chip, t + 1, chips)
        landed = recvbuf.at[0]
        pltpu.make_async_copy(landed, landed, strip_recv_sem.at[t]).wait()
        for half in range(STRIPS // 8):

            def count(role):
                at = there * pool + role * STRIPS + half * 8
                return rcnt[pl.ds(pl.multiple_of(at, 8), 8), :]

            def block(p):
                return recvbuf[there, half * 8 : half * 8 + 8, p * LANES : (p + 1) * LANES]

            for outer, inner, at in ((0, 1, lambda p: p), (3, 2, lambda p: STRIP_BLOCKS - 1 - p)):
                top = outer * STRIPS + half * 8
                for j in range(nblocks):
                    roles[top : top + 8, j * LANES : (j + 1) * LANES] = block(at(j))
                behind = [block(at(p)) for p in range(reach)]
                behind = shifted_down(behind, shift_bits(count(outer)), nblocks)
                top = inner * STRIPS + half * 8
                for j in range(nblocks):
                    roles[top : top + 8, j * LANES : (j + 1) * LANES] = behind[j]
        order = undeal[there][:, :pool]
        for c in range(1, CHUNKS):
            out = permuted(order, roles[:, (c - 1) * width : c * width])
            for r in range(2 * members_dev):
                finish_rows(there * 2 * members_dev + r, c * width, out[r * part : (r + 1) * part])

    def unpack_step(t, carry):
        unpack(t)
        return carry

    lax.fori_loop(0, 2, unpack_step, 0)

    for copy in tail_copies:
        copy.wait()
    ends = tails_recv[...]
    needs[0] = jnp.max(ends, axis=0)
    need_copies = axis_sends(needs, need_send_sem, need_recv_sem)
    for copy in need_copies:
        copy.start()
    first_sum = column_in(ends, 0).reshape(members, part, 1)
    second_sum = column_in(ends, 1).reshape(members, part, 1)
    value = (second_sum - advantage * first_sum) * (samples / ntok)[None]
    shape = (members, part, LANES)
    spread = lax.broadcasted_iota(jnp.int32, shape, 1) == lax.broadcasted_iota(jnp.int32, shape, 2)
    loss_ref[...] = jnp.sum(jnp.where(spread, value, 0.0), axis=1)[:, :part]
    adv_ref[...] = jnp.sum(jnp.where(spread, advantage, 0.0), axis=1)[:, :part]
    for copy in need_copies:
        copy.wait()
    fullest = needs[0]
    for off in range(1, n_gx):
        fullest = jnp.maximum(fullest, needs[off])
    over_ref[0, 0] = (jnp.max(fullest[:, fill_lane : fill_lane + 1]) > STRIP_BLOCKS).astype(jnp.int32)
    for copy in first_copies:
        copy.wait_send()
    pltpu.make_async_copy(got, got, give_send_sem).wait()

    unpack(chips - 2)
    for t in range(chips - 1):
        sent = sendbuf.at[0]
        pltpu.make_async_copy(sent, sent, strip_send_sem.at[t]).wait()


def store(done, loss, adv, grad, loss_out, adv_out, sem):
    copies = [
        pltpu.make_async_copy(src, dst, sem.at[k])
        for k, (src, dst) in enumerate(((done, grad), (loss, loss_out), (adv, adv_out)))
    ]
    for copy in copies:
        copy.start()
    for copy in copies:
        copy.wait()


def packed_body(n_gx, n_gy, policy_logp, anchor_logp, lengths, rewards, slot_prompt):
    members_dev, slots, seq = policy_logp.shape
    members, part = members_dev * n_gy, slots // n_gy
    f32, bf16 = jnp.float32, jnp.bfloat16
    chips, rows = n_gy // 2, members_dev * part
    pool = 2 * rows
    width = seq // CHUNKS
    chunked = (CHUNKS, members_dev, slots, width)
    strips = (chips, STRIPS, STRIP_BLOCKS * LANES)
    per_slot = (members_dev, slots, LANES)
    per_sample = (members, part, LANES)
    tile = (n_gy, 8, LANES)
    hbm_spec = pl.BlockSpec(memory_space=pltpu.HBM)
    vmem_spec = pl.BlockSpec(memory_space=pltpu.VMEM)
    dma = pltpu.SemaphoreType.DMA
    done, loss, adv, over = pl.pallas_call(
        functools.partial(packed_exchange, n_gx, n_gy),
        out_shape=(
            pltpu.VMEM((members, part, seq), f32),
            pltpu.VMEM((members, part), f32),
            pltpu.VMEM((members, part), f32),
            jax.ShapeDtypeStruct((1, 1), jnp.int32),
        ),
        in_specs=[hbm_spec] * 5,
        out_specs=(vmem_spec,) * 3 + (pl.BlockSpec(memory_space=pltpu.SMEM),),
        scratch_shapes=[
            pltpu.VMEM(chunked, f32),
            pltpu.VMEM(chunked, f32),
            pltpu.VMEM((members_dev, slots), jnp.int32),
            pltpu.VMEM((members_dev, slots), jnp.int32),
            pltpu.VMEM((members_dev, slots), jnp.int32),
            pltpu.VMEM((2 * chips * rows, members_dev * slots), bf16),
            pltpu.VMEM((2, chips, rows, seq), f32),
            pltpu.VMEM((chips, rows, seq), f32),
            pltpu.VMEM((n_gy, rows, width), f32),
            pltpu.VMEM(strips, f32),
            pltpu.VMEM(strips, f32),
            pltpu.VMEM((pool, seq - width), f32),
            pltpu.VMEM((chips, pool, pool), bf16),
            pltpu.VMEM((chips, pool, LANES), bf16),
            pltpu.VMEM((chips * pool, LANES), f32),
            pltpu.VMEM((chips * pool, LANES), f32),
            pltpu.VMEM(per_slot, f32),
            pltpu.VMEM(per_slot, f32),
            pltpu.VMEM(per_slot, f32),
            pltpu.VMEM(per_sample, f32),
            pltpu.VMEM(per_sample, f32),
            pltpu.VMEM(tile, f32),
            pltpu.VMEM((chips, 8, LANES), f32),
            pltpu.VMEM(tile, f32),
            pltpu.VMEM(tile, f32),
            pltpu.VMEM(tile, f32),
            pltpu.VMEM((n_gx, 8, LANES), f32),
            pltpu.VMEM((n_gx, 8, LANES), f32),
            dma((3,)),
            dma((2, CHUNKS)),
            dma(()),
            dma(()),
            dma((n_gy - 2,)),
            dma((n_gy - 2,)),
            dma((chips - 1,)),
            dma((chips - 1,)),
            dma((n_gy - 1,)),
            dma((n_gy - 1,)),
            dma((n_gy - 1,)),
            dma((n_gy - 1,)),
            dma((n_gx - 1,)),
            dma((n_gx - 1,)),
            dma((n_gx - 1,)),
            dma((n_gx - 1,)),
        ],
        compiler_params=pltpu.CompilerParams(collective_id=0, has_side_effects=True, vmem_limit_bytes=56 * 2**20),
    )(policy_logp, anchor_logp, lengths, rewards, slot_prompt)

    def fits(policy_logp, anchor_logp, lengths, rewards, slot_prompt, done, loss, adv):
        small = jax.ShapeDtypeStruct((members, part), f32)
        return tuple(pl.pallas_call(
            store,
            out_shape=(jax.ShapeDtypeStruct((members, part, seq), f32), small, small),
            in_specs=[vmem_spec] * 3,
            out_specs=(hbm_spec,) * 3,
            scratch_shapes=[dma((3,))],
            compiler_params=pltpu.CompilerParams(vmem_limit_bytes=16 * 2**20),
        )(done, loss, adv))

    def overflows(policy_logp, anchor_logp, lengths, rewards, slot_prompt, done, loss, adv):
        return tuple(unpacked_body(n_gx, n_gy, policy_logp, anchor_logp, lengths, rewards, slot_prompt))

    return lax.cond(
        over[0, 0] > 0, overflows, fits,
        policy_logp, anchor_logp, lengths, rewards, slot_prompt, done, loss, adv,
    )


def body(n_gx, n_gy, *args):
    members_dev, slots, seq = args[0].shape
    pool = 2 * members_dev * slots // n_gy
    packs = n_gy == 8 and pool == ROLES * STRIPS and slots == LANES and seq == LANES * 32 and seq == CHUNKS * HEAD_BLOCKS * LANES
    return (packed_body if packs else unpacked_body)(n_gx, n_gy, *args)


def solution(mesh):
    placed = (P("gy", "gx", None), P("gy", "gx", None), P("gy", "gx"), P("gy", "gx"), P("gy", "gx"))
    return jax.shard_map(
        functools.partial(body, mesh.shape["gx"], mesh.shape["gy"]),
        mesh=mesh,
        in_specs=placed,
        out_specs=(P(None, ("gx", "gy"), None), P(None, ("gx", "gy")), P(None, ("gx", "gy"))),
        check_vma=False,
    )
```

profile of v0, /device:TPU:0, one launch (start us, length us, event | category | flops | bytes accessed | tf_op | source)
XLA Modules:
  0.0 48.4 jit_solution(12677380513276436482)
XLA Ops:
  0.6 0.0 copy-start
  0.6 0.0 copy-start.1
  0.7 0.0 copy-start.2
  0.7 45.1 %shard_map.82 = (f32[16,16,4096]{2,1,0:T(8,128)S(1)}, f32[16,16]{1,0:T(8,128)S(1)}, f32[16,16]{1,0:T(8,128)S(1)}, s32[1,1]{1,0:T(1,128)}) custom-call(f32[2,128,4096]{2,1,0:T(8,128)} %policy_hbm.1, f32[2,128,4096]{2,1,0:T(8,128)} %anchor_hbm.1, s32[2,128]{1,0:T(2,128)} %len_hbm.1, s32[2,128]{1,0:T(2,128)} %reward_hbm.1, s32[2,128]{1,0:T(2,128)} %prompt_hbm.1), custom_call_target="tpu_custom_call" | custom-call | tf_op jit(solution)/shard_map/pallas_call | solution.py:829
  46.3 0.0 copy-done
  46.3 0.0 copy-done.1
  46.3 0.0 copy-done.2
  46.3 2.1 %conditional.1 = ((f32[16,16,4096]{2,1,0:T(8,128)}, f32[16,16]{1,0:T(8,128)}, f32[16,16]{1,0:T(8,128)})) conditional(s32[]{:T(128)} %bitcast, (f32[16,16,4096]{2,1,0:T(8,128)S(1)}, f32[16,16]{1,0:T(8,128)S(1)}, f32[16,16]{1,0:T(8,128)S(1)}) %tuple.13, (f32[2,128,4096]{2,1,0:T(8,128)}, f32[2,128,4096]{2,1,0:T(8,128)}, s32[2,128]{1,0:T(2,128)S(1)}, ...), branch_computations={%region_0.0_spmd, %region_1.0_spmd} | conditional | bytes 8 | solution.py:902
  46.4 2.0 %branch_0_fun.1 = (f32[16,16,4096]{2,1,0:T(8,128)}, f32[16,16]{1,0:T(8,128)}, f32[16,16]{1,0:T(8,128)}) custom-call(f32[16,16,4096]{2,1,0:T(8,128)S(1)} %get-tuple-element.16.done, f32[16,16]{1,0:T(8,128)S(1)} %get-tuple-element.17.loss, f32[16,16]{1,0:T(8,128)S(1)} %get-tuple-element.18.adv), custom_call_target="tpu_custom_call" | custom-call | tf_op jit(solution)/shard_map/cond/branch_0_fun/pallas_call | solution.py:890
Async XLA Ops:
  0.6 45.7 %copy-start = (s32[2,128]{1,0:T(2,128)S(1)}, s32[2,128]{1,0:T(2,128)}, u32[]{:S(2)}) copy-start(s32[2,128]{1,0:T(2,128)} %len_hbm.1) | copy-start | bytes 3076
  0.6 45.7 %copy-start.1 = (s32[2,128]{1,0:T(2,128)S(1)}, s32[2,128]{1,0:T(2,128)}, u32[]{:S(2)}) copy-start(s32[2,128]{1,0:T(2,128)} %reward_hbm.1) | copy-start | bytes 3076
  0.7 45.7 %copy-start.2 = (s32[2,128]{1,0:T(2,128)S(1)}, s32[2,128]{1,0:T(2,128)}, u32[]{:S(2)}) copy-start(s32[2,128]{1,0:T(2,128)} %prompt_hbm.1) | copy-start | bytes 3076
where the time goes:
time: 48.7 us; the launch traced here: 48.4 us
  Pallas kernels  47.1 us (97%)
  between operations  1.25 us (3%)
    pallas_call x1, Pallas kernels, packed_body(): pl.pallas_call(functools.partial(packed_exchange, n_gx, n_gy), out_shape=...  45.1 us
    pallas_call x1, Pallas kernels, fits(): pl.pallas_call(store, out_shape=(jax.ShapeDtypeStruct((members, part, seq...  2.05 us

commit v1 on v0

--- a/solution.py
+++ b/solution.py
@@ -15,7 +15,7 @@
 STRIPS = 16
 SHIFTS = 5
 HEAD_BLOCKS = 4
-STRIP_BLOCKS = 75
+STRIP_BLOCKS = 74
 FIRST_ORDER = (2, 4, 3, 5, 6, 7)
 
 
@@ -331,9 +331,11 @@
 def strip_spot(rank):
     first, second, third = rank < STRIPS, rank < 2 * STRIPS, rank < 3 * STRIPS
     strip = jnp.where(
-        first, rank, jnp.where(second, 2 * STRIPS - 1 - rank, jnp.where(third, rank - 2 * STRIPS, 4 * STRIPS - 1 - rank))
+        first, rank, jnp.where(second, 2 * STRIPS - 1 - rank, jnp.where(third, 3 * STRIPS - 1 - rank, rank - 3 * STRIPS))
     )
-    return jnp.where(first, 0.0, jnp.where(second, 3.0, jnp.where(third, 2.0, 1.0))) * STRIPS + strip
+    role = jnp.where(first, 0.0, jnp.where(second, 3.0, jnp.where(third, 2.0, 1.0)))
+    half = jnp.floor(strip * (1.0 / 8))
+    return half * (ROLES * 8) + role * 8 + strip - half * 8
 
 
 def strip_plan(len_row, len_column, group_row, group_column, index_row, index_column, n_groups, seq):
@@ -395,7 +397,7 @@
     n_gx, n_gy, policy_hbm, anchor_hbm, len_hbm, reward_hbm, prompt_hbm,
     done, loss_ref, adv_ref, over_ref,
     policy, anchor, len_ref, reward_ref, prompt_ref, onehot, ordered, got, heads_in, sendbuf, recvbuf, roles,
-    deal, undeal, cnt, rcnt, len_col, sum_policy, sum_kl, len_rows, adv_rows,
+    deal, undeal, cnt, rcnt, len_col, sum_policy, sum_kl, len_rows, adv_rows, half_rows,
     info_send, info_got, info_recv, tails_send, tails_recv, counts, needs,
     small_sem, load_sem, give_send_sem, give_recv_sem, first_send_sem, first_recv_sem, strip_send_sem, strip_recv_sem,
     info_send_sem, info_recv_sem, tail_send_sem, tail_recv_sem, count_send_sem, count_recv_sem, need_send_sem, need_recv_sem,
@@ -462,16 +464,26 @@
         cols = pl.ds(pl.multiple_of(c * width, LANES), width)
         ordered[:, :, :, cols] = out.reshape(2, chips, rows, width)
 
-    def give(c):
+    def give(c, there):
         cols = pl.ds(pl.multiple_of(c * width, LANES), width)
         return pltpu.make_async_remote_copy(
-            src_ref=ordered.at[1, :, :, cols],
-            dst_ref=got.at[:, :, cols],
-            send_sem=give_send_sem,
-            recv_sem=give_recv_sem,
+            src_ref=ordered.at[1, there, :, cols],
+            dst_ref=got.at[there, :, cols],
+            send_sem=give_send_sem.at[0],
+            recv_sem=give_recv_sem.at[0],
             device_id=(gx, mate),
             device_id_type=MESH,
         )
+
+    give_own = pltpu.make_async_remote_copy(
+        src_ref=ordered.at[1, chip],
+        dst_ref=got.at[chip],
+        send_sem=give_send_sem.at[1],
+        recv_sem=give_recv_sem.at[1],
+        device_id=(gx, mate),
+        device_id_type=MESH,
+    )
+    given = got.at[pl.ds(0, chips - 1), :, pl.ds(width, seq - width)]
 
     def first_send(off):
         peer = partner(gy, off, n_gy)
@@ -489,7 +501,6 @@
     first_copies = [first_send(off) for off in FIRST_ORDER]
     for copy in first_copies:
         copy.start()
-    give(0).start()
 
     tile_lane = lax.broadcasted_iota(jnp.int32, (n_gy, 8, LANES), 2)
     groups = rows // 8
@@ -542,10 +553,12 @@
 
     def order_step(c, carry):
         put_in_order(c)
-        give(c).start()
+        for t in range(1, chips):
+            give(c, peer_of(chip, t, chips)).start()
         return carry
 
     lax.fori_loop(1, CHUNKS, order_step, 0)
+    give_own.start()
 
     mate_info.wait()
     pair_lens = jnp.concatenate(
@@ -570,40 +583,43 @@
 
     pair_counts = strip_counts(spot_row, pair_row)
     cnt[...] = jnp.broadcast_to(pair_counts, cnt.shape)
-    fill = jnp.sum(pair_counts.reshape(chips, ROLES, STRIPS, 1), axis=1)
-    sent_chip = lax.broadcasted_iota(jnp.int32, (chips, STRIPS, 1), 0) != chip
+    fill = jnp.sum(pair_counts.reshape(chips, STRIPS // 8, ROLES, 8, 1), axis=2)
+    sent_chip = lax.broadcasted_iota(jnp.int32, fill.shape, 0) != chip
     local_fill = jnp.max(jnp.where(sent_chip, fill, 0.0))
     square = lax.broadcasted_iota(jnp.int32, (pool, pool), 0).astype(f32)
     for s in range(chips):
         deal[s] = jnp.where(square == spot_row[:, s * pool : (s + 1) * pool], 1.0, 0.0).astype(jnp.bfloat16)
-    pltpu.make_async_copy(got, got, give_recv_sem).wait()
-
-    def strip_send(t, there):
-        return pltpu.make_async_remote_copy(
-            src_ref=sendbuf.at[there],
-            dst_ref=recvbuf.at[chip],
-            send_sem=strip_send_sem.at[t],
-            recv_sem=strip_recv_sem.at[t],
-            device_id=(gx, there * 2 + core),
-            device_id_type=MESH,
-        )
+    pltpu.make_async_copy(given, given, give_recv_sem.at[0]).wait()
+
+    def strip_sends(t, there):
+        return [
+            pltpu.make_async_remote_copy(
+                src_ref=sendbuf.at[there, half],
+                dst_ref=recvbuf.at[chip, half],
+                send_sem=strip_send_sem.at[t, half],
+                recv_sem=strip_recv_sem.at[t, half],
+                device_id=(gx, there * 2 + core),
+                device_id_type=MESH,
+            )
+            for half in range(STRIPS // 8)
+        ]
 
     reach = 2 * nblocks
 
-    def pack(there):
+    def pack(t, there):
         for c in range(1, CHUNKS):
             both = jnp.concatenate(
                 [ordered[0, there, :, c * width : (c + 1) * width], got[there, :, c * width : (c + 1) * width]], axis=0
             )
             roles[:, (c - 1) * width : c * width] = permuted(deal[there], both)
-        for half in range(STRIPS // 8):
+        for half, copy in enumerate(strip_sends(t, there)):
 
             def count(role):
-                at = there * pool + role * STRIPS + half * 8
+                at = there * pool + half * ROLES * 8 + role * 8
                 return cnt[pl.ds(pl.multiple_of(at, 8), 8), :]
 
             def blocks(role):
-                at = role * STRIPS + half * 8
+                at = half * ROLES * 8 + role * 8
                 return [roles[at : at + 8, j * LANES : (j + 1) * LANES] for j in range(nblocks)]
 
             def side(outer, inner):
@@ -622,16 +638,20 @@
                     value = right[q]
                 else:
                     value = jnp.where(left_n > p, left[p], right[q])
-                sendbuf[there, half * 8 : half * 8 + 8, p * LANES : (p + 1) * LANES] = value
+                sendbuf[there, half, :, p * LANES : (p + 1) * LANES] = value
 
     def near_step(t, carry):
         there = peer_of(chip, t + 1, chips)
-        pack(there)
-        strip_send(t, there).start()
+        pack(t, there)
         return carry
 
+    far = peer_of(chip, chips - 1, chips)
+    pack(chips - 2, far)
+    for copy in strip_sends(chips - 2, far):
+        copy.start()
+
+
     lax.fori_loop(0, 2, near_step, 0)
-
     info_recv[gy] = info_send[chip]
     for copy in info_copies[1:]:
         copy.wait()
@@ -684,9 +704,11 @@
         copy.start()
     tails_recv[gy] = tails_send[chip]
 
-    far = peer_of(chip, chips - 1, chips)
-    pack(far)
-    strip_send(chips - 2, far).start()
+    near_copies = [strip_sends(t, peer_of(chip, t + 1, chips)) for t in range(2)]
+    for half in range(2):
+        for t in range(2):
+            near_copies[t][half].start()
+
 
     for copy in count_copies:
         copy.wait()
@@ -706,14 +728,21 @@
         lax.rem(row, pool).astype(f32), lax.rem(column, pool).astype(f32), chips, seq,
     )
     rcnt[...] = jnp.broadcast_to(strip_counts(got_spot_row, got_row), rcnt.shape)
-    pick = got_spot == lax.broadcasted_iota(jnp.int32, (total_rows, LANES), 1).astype(f32)
-    undeal[...] = jnp.where(pick, 1.0, 0.0).astype(jnp.bfloat16).reshape(chips, pool, LANES)
+    lane = lax.broadcasted_iota(jnp.int32, (total_rows, LANES), 1).astype(f32)
+    for half in range(STRIPS // 8):
+        pick = got_spot - half * ROLES * 8 == lane
+        pick = jnp.where(pick & (lane < ROLES * 8), 1.0, 0.0).astype(jnp.bfloat16)
+        undeal[:, half] = pick.reshape(chips, pool, LANES)
+    half_rows[...] = jnp.broadcast_to(jnp.where(got_spot < ROLES * 8, 0.0, 1.0).reshape(members, part, 1), half_rows.shape)
     lane_width = lax.broadcasted_iota(jnp.int32, (part, width), 1).astype(f32)
 
-    def finish_rows(k, start, value):
+    def finish_rows(k, start, value, only=None):
         value = (value - adv_rows[k][:, :1]) * scale
         valid = lane_width < len_rows[k][:, :1] - start
-        done[k, :, start : start + width] = jnp.where(valid, value, 0.0)
+        value = jnp.where(valid, value, 0.0)
+        if only is not None:
+            value = jnp.where(only, value, done[k, :, start : start + width])
+        done[k, :, start : start + width] = value
 
     def own_step(which, source):
         for m in range(members_dev):
@@ -721,6 +750,7 @@
                 finish_rows(source * members_dev + m, c * width, which(m * part, c * width))
 
     own_step(lambda r, s: ordered[0, chip, r : r + part, s : s + width], gy)
+    give_own.wait_recv()
     own_step(lambda r, s: got[chip, r : r + part, s : s + width], mate)
 
     def first_wait(off):
@@ -736,39 +766,39 @@
 
     lax.fori_loop(2, n_gy, first_step, 0)
 
-    def unpack(t):
+    def unpack(t, half):
         there = peer_of(chip, t + 1, chips)
-        landed = recvbuf.at[0]
-        pltpu.make_async_copy(landed, landed, strip_recv_sem.at[t]).wait()
+        landed = recvbuf.at[0, 0]
+        pltpu.make_async_copy(landed, landed, strip_recv_sem.at[t, half]).wait()
+
+        def count(role):
+            at = there * pool + half * ROLES * 8 + role * 8
+            return rcnt[pl.ds(pl.multiple_of(at, 8), 8), :]
+
+        def block(p):
+            return recvbuf[there, half, :, p * LANES : (p + 1) * LANES]
+
+        for outer, inner, at in ((0, 1, lambda p: p), (3, 2, lambda p: STRIP_BLOCKS - 1 - p)):
+            for j in range(nblocks):
+                roles[outer * 8 : outer * 8 + 8, j * LANES : (j + 1) * LANES] = block(at(j))
+            behind = [block(at(p)) for p in range(reach)]
+            behind = shifted_down(behind, shift_bits(count(outer)), nblocks)
+            for j in range(nblocks):
+                roles[inner * 8 : inner * 8 + 8, j * LANES : (j + 1) * LANES] = behind[j]
+        order = undeal[there, half][:, : ROLES * 8]
+        for c in range(1, CHUNKS):
+            out = permuted(order, roles[: ROLES * 8, (c - 1) * width : c * width])
+            for r in range(2 * members_dev):
+                k = there * 2 * members_dev + r
+                finish_rows(k, c * width, out[r * part : (r + 1) * part], half_rows[k][:, :1] > 0.5 if half else None)
+
+    def unpack_step(t, carry):
         for half in range(STRIPS // 8):
-
-            def count(role):
-                at = there * pool + role * STRIPS + half * 8
-                return rcnt[pl.ds(pl.multiple_of(at, 8), 8), :]
-
-            def block(p):
-                return recvbuf[there, half * 8 : half * 8 + 8, p * LANES : (p + 1) * LANES]
-
-            for outer, inner, at in ((0, 1, lambda p: p), (3, 2, lambda p: STRIP_BLOCKS - 1 - p)):
-                top = outer * STRIPS + half * 8
-                for j in range(nblocks):
-                    roles[top : top + 8, j * LANES : (j + 1) * LANES] = block(at(j))
-                behind = [block(at(p)) for p in range(reach)]
-                behind = shifted_down(behind, shift_bits(count(outer)), nblocks)
-                top = inner * STRIPS + half * 8
-                for j in range(nblocks):
-                    roles[top : top + 8, j * LANES : (j + 1) * LANES] = behind[j]
-        order = undeal[there][:, :pool]
-        for c in range(1, CHUNKS):
-            out = permuted(order, roles[:, (c - 1) * width : c * width])
-            for r in range(2 * members_dev):
-                finish_rows(there * 2 * members_dev + r, c * width, out[r * part : (r + 1) * part])
-
-    def unpack_step(t, carry):
-        unpack(t)
+            unpack(t, half)
         return carry
 
-    lax.fori_loop(0, 2, unpack_step, 0)
+    for half in range(STRIPS // 8):
+        unpack(chips - 2, half)
 
     for copy in tail_copies:
         copy.wait()
@@ -792,12 +822,14 @@
     over_ref[0, 0] = (jnp.max(fullest[:, fill_lane : fill_lane + 1]) > STRIP_BLOCKS).astype(jnp.int32)
     for copy in first_copies:
         copy.wait_send()
-    pltpu.make_async_copy(got, got, give_send_sem).wait()
-
-    unpack(chips - 2)
+    pltpu.make_async_copy(given, given, give_send_sem.at[0]).wait()
+    give_own.wait_send()
+
+    lax.fori_loop(0, 2, unpack_step, 0)
     for t in range(chips - 1):
-        sent = sendbuf.at[0]
-        pltpu.make_async_copy(sent, sent, strip_send_sem.at[t]).wait()
+        for half in range(STRIPS // 8):
+            sent = sendbuf.at[0, 0]
+            pltpu.make_async_copy(sent, sent, strip_send_sem.at[t, half]).wait()
 
 
 def store(done, loss, adv, grad, loss_out, adv_out, sem):
@@ -819,7 +851,7 @@
     pool = 2 * rows
     width = seq // CHUNKS
     chunked = (CHUNKS, members_dev, slots, width)
-    strips = (chips, STRIPS, STRIP_BLOCKS * LANES)
+    strips = (chips, STRIPS // 8, 8, STRIP_BLOCKS * LANES)
     per_slot = (members_dev, slots, LANES)
     per_sample = (members, part, LANES)
     tile = (n_gy, 8, LANES)
@@ -832,7 +864,7 @@
             pltpu.VMEM((members, part, seq), f32),
             pltpu.VMEM((members, part), f32),
             pltpu.VMEM((members, part), f32),
-            jax.ShapeDtypeStruct((1, 1), jnp.int32),
+            pltpu.SMEM((1, 1), jnp.int32),
         ),
         in_specs=[hbm_spec] * 5,
         out_specs=(vmem_spec,) * 3 + (pl.BlockSpec(memory_space=pltpu.SMEM),),
@@ -850,12 +882,13 @@
             pltpu.VMEM(strips, f32),
             pltpu.VMEM((pool, seq - width), f32),
             pltpu.VMEM((chips, pool, pool), bf16),
-            pltpu.VMEM((chips, pool, LANES), bf16),
+            pltpu.VMEM((chips, STRIPS // 8, pool, LANES), bf16),
             pltpu.VMEM((chips * pool, LANES), f32),
             pltpu.VMEM((chips * pool, LANES), f32),
             pltpu.VMEM(per_slot, f32),
             pltpu.VMEM(per_slot, f32),
             pltpu.VMEM(per_slot, f32),
+            pltpu.VMEM(per_sample, f32),
             pltpu.VMEM(per_sample, f32),
             pltpu.VMEM(per_sample, f32),
             pltpu.VMEM(tile, f32),
@@ -867,12 +900,12 @@
             pltpu.VMEM((n_gx, 8, LANES), f32),
             dma((3,)),
             dma((2, CHUNKS)),
-            dma(()),
-            dma(()),
+            dma((2,)),
+            dma((2,)),
             dma((n_gy - 2,)),
             dma((n_gy - 2,)),
-            dma((chips - 1,)),
-            dma((chips - 1,)),
+            dma((chips - 1, STRIPS // 8)),
+            dma((chips - 1, STRIPS // 8)),
             dma((n_gy - 1,)),
             dma((n_gy - 1,)),
             dma((n_gy - 1,)),

time: 48.7 us -> 44.6 us (0.916)
  Pallas kernels: 47.1 us -> 43.7 us
  between operations: 1.25 us -> 0.69 us
    pallas_call x1, Pallas kernels: 45.1 us -> 41.7 us  [packed_body(): pl.pallas_call(functools.partial(packed_exchange, n_gx, n_gy), out_shape=...]
where the time goes in v1:
time: 44.6 us; the launch traced here: 44.4 us
  Pallas kernels  43.7 us (98%)
  between operations  0.69 us (2%)
    pallas_call x1, Pallas kernels, packed_body(): pl.pallas_call(functools.partial(packed_exchange, n_gx, n_gy), out_shape=...  41.7 us
    pallas_call x1, Pallas kernels, fits(): pl.pallas_call(store, out_shape=(jax.ShapeDtypeStruct((members, part, seq...  2.05 us

profile of v1, /device:TPU:0, one launch (start us, length us, event | category | flops | bytes accessed | tf_op | source)
XLA Modules:
  0.0 44.4 jit_solution(17326613505857577501)
XLA Ops:
  0.6 0.0 copy-start
  0.6 0.0 copy-start.1
  0.7 0.0 copy-start.2
  0.7 41.7 %shard_map.82 = (f32[16,16,4096]{2,1,0:T(8,128)S(1)}, f32[16,16]{1,0:T(8,128)S(1)}, f32[16,16]{1,0:T(8,128)S(1)}, s32[1,1]{1,0:T(1,128)S(4)}) custom-call(f32[2,128,4096]{2,1,0:T(8,128)} %policy_hbm.1, f32[2,128,4096]{2,1,0:T(8,128)} %anchor_hbm.1, s32[2,128]{1,0:T(2,128)} %len_hbm.1, s32[2,128]{1,0:T(2,128)} %reward_hbm.1, s32[2,128]{1,0:T(2,128)} %prompt_hbm.1), custom_call_target="tpu_custom_call" | custom-call | tf_op jit(solution)/shard_map/pallas_call | solution.py:861
  42.3 0.0 copy-done
  42.4 0.0 copy-done.1
  42.4 0.0 copy-done.2
  42.4 2.1 %conditional.1 = ((f32[16,16,4096]{2,1,0:T(8,128)}, f32[16,16]{1,0:T(8,128)}, f32[16,16]{1,0:T(8,128)})) conditional(s32[]{:T(128)} %bitcast, (f32[16,16,4096]{2,1,0:T(8,128)S(1)}, f32[16,16]{1,0:T(8,128)S(1)}, f32[16,16]{1,0:T(8,128)S(1)}) %tuple.13, (f32[2,128,4096]{2,1,0:T(8,128)}, f32[2,128,4096]{2,1,0:T(8,128)}, s32[2,128]{1,0:T(2,128)S(1)}, ...), branch_computations={%region_0.0_spmd, %region_1.0_spmd} | conditional | bytes 8 | solution.py:935
  42.4 2.0 %branch_0_fun.1 = (f32[16,16,4096]{2,1,0:T(8,128)}, f32[16,16]{1,0:T(8,128)}, f32[16,16]{1,0:T(8,128)}) custom-call(f32[16,16,4096]{2,1,0:T(8,128)S(1)} %get-tuple-element.16.done, f32[16,16]{1,0:T(8,128)S(1)} %get-tuple-element.17.loss, f32[16,16]{1,0:T(8,128)S(1)} %get-tuple-element.18.adv), custom_call_target="tpu_custom_call" | custom-call | tf_op jit(solution)/shard_map/cond/branch_0_fun/pallas_call | solution.py:923
Async XLA Ops:
  0.6 41.7 %copy-start = (s32[2,128]{1,0:T(2,128)S(1)}, s32[2,128]{1,0:T(2,128)}, u32[]{:S(2)}) copy-start(s32[2,128]{1,0:T(2,128)} %len_hbm.1) | copy-start | bytes 3076
  0.6 41.7 %copy-start.1 = (s32[2,128]{1,0:T(2,128)S(1)}, s32[2,128]{1,0:T(2,128)}, u32[]{:S(2)}) copy-start(s32[2,128]{1,0:T(2,128)} %reward_hbm.1) | copy-start | bytes 3076
  0.7 41.7 %copy-start.2 = (s32[2,128]{1,0:T(2,128)S(1)}, s32[2,128]{1,0:T(2,128)}, u32[]{:S(2)}) copy-start(s32[2,128]{1,0:T(2,128)} %prompt_hbm.1) | copy-start | bytes 3076

commit v2 on v1

--- a/solution.py
+++ b/solution.py
@@ -13,6 +13,7 @@
 MESH = pl.DeviceIdType.MESH
 ROLES = 4
 STRIPS = 16
+HALVES = STRIPS // 8
 SHIFTS = 5
 HEAD_BLOCKS = 4
 STRIP_BLOCKS = 74
@@ -297,7 +298,7 @@
             dma((n_gx - 1,)),
             dma((n_gx - 1,)),
         ],
-        compiler_params=pltpu.CompilerParams(collective_id=1, has_side_effects=True, vmem_limit_bytes=56 * 2**20),
+        compiler_params=pltpu.CompilerParams(collective_id=1, has_side_effects=True, vmem_limit_bytes=36 * 2**20),
     )(policy_logp, anchor_logp, lengths, rewards, slot_prompt)
     samples = members * slots * n_gx
     return pl.pallas_call(
@@ -393,13 +394,38 @@
     return out
 
 
+def unpack_strips(recvbuf, roles, undeal, rcnt, there, half, width, part, put):
+    pool, seq_tail = undeal.shape[2], roles.shape[1]
+    nblocks = seq_tail // LANES
+
+    def count(role):
+        at = there * pool + half * ROLES * 8 + role * 8
+        return rcnt[pl.ds(pl.multiple_of(at, 8), 8), :]
+
+    def block(p):
+        return recvbuf[there, half, :, p * LANES : (p + 1) * LANES]
+
+    for outer, inner, at in ((0, 1, lambda p: p), (3, 2, lambda p: STRIP_BLOCKS - 1 - p)):
+        for j in range(nblocks):
+            roles[outer * 8 : outer * 8 + 8, j * LANES : (j + 1) * LANES] = block(at(j))
+        behind = [block(at(p)) for p in range(2 * nblocks)]
+        behind = shifted_down(behind, shift_bits(count(outer)), nblocks)
+        for j in range(nblocks):
+            roles[inner * 8 : inner * 8 + 8, j * LANES : (j + 1) * LANES] = behind[j]
+    order = undeal[there, half][:, : ROLES * 8]
+    for c in range(seq_tail // width):
+        out = permuted(order, roles[: ROLES * 8, c * width : (c + 1) * width])
+        for r in range(pool // part):
+            put(r, c + 1, out[r * part : (r + 1) * part])
+
+
 def packed_exchange(
     n_gx, n_gy, policy_hbm, anchor_hbm, len_hbm, reward_hbm, prompt_hbm,
-    done, loss_ref, adv_ref, over_ref,
-    policy, anchor, len_ref, reward_ref, prompt_ref, onehot, ordered, got, heads_in, sendbuf, recvbuf, roles,
-    deal, undeal, cnt, rcnt, len_col, sum_policy, sum_kl, len_rows, adv_rows, half_rows,
+    done, loss_ref, adv_ref, over_ref, recvbuf, undeal, rcnt, len_rows, adv_rows, half_rows, scale_ref,
+    policy, anchor, len_ref, reward_ref, prompt_ref, onehot, ordered, got, heads_in, sendbuf, passing, roles,
+    deal, cnt, len_col, sum_policy, sum_kl,
     info_send, info_got, info_recv, tails_send, tails_recv, counts, needs,
-    small_sem, load_sem, give_send_sem, give_recv_sem, first_send_sem, first_recv_sem, strip_send_sem, strip_recv_sem,
+    small_sem, load_sem, give_send_sem, give_recv_sem, first_send_sem, first_recv_sem, strip_send_sem, strip_recv_sem, first_leg_send_sem, first_leg_recv_sem,
     info_send_sem, info_recv_sem, tail_send_sem, tail_recv_sem, count_send_sem, count_recv_sem, need_send_sem, need_recv_sem,
 ):
     gx, gy = lax.axis_index("gx"), lax.axis_index("gy")
@@ -583,7 +609,7 @@
 
     pair_counts = strip_counts(spot_row, pair_row)
     cnt[...] = jnp.broadcast_to(pair_counts, cnt.shape)
-    fill = jnp.sum(pair_counts.reshape(chips, STRIPS // 8, ROLES, 8, 1), axis=2)
+    fill = jnp.sum(pair_counts.reshape(chips, HALVES, ROLES, 8, 1), axis=2)
     sent_chip = lax.broadcasted_iota(jnp.int32, fill.shape, 0) != chip
     local_fill = jnp.max(jnp.where(sent_chip, fill, 0.0))
     square = lax.broadcasted_iota(jnp.int32, (pool, pool), 0).astype(f32)
@@ -591,28 +617,33 @@
         deal[s] = jnp.where(square == spot_row[:, s * pool : (s + 1) * pool], 1.0, 0.0).astype(jnp.bfloat16)
     pltpu.make_async_copy(given, given, give_recv_sem.at[0]).wait()
 
-    def strip_sends(t, there):
+    chip_x, chip_y = peer_of(chip, 1, chips), peer_of(chip, 2, chips)
+
+    def relay(src, dst, there, send, recv, half):
+        return pltpu.make_async_remote_copy(
+            src_ref=src,
+            dst_ref=dst,
+            send_sem=send.at[half],
+            recv_sem=recv.at[half],
+            device_id=(gx, there * 2 + core),
+            device_id_type=MESH,
+        )
+
+    def near_sends(there, t):
         return [
-            pltpu.make_async_remote_copy(
-                src_ref=sendbuf.at[there, half],
-                dst_ref=recvbuf.at[chip, half],
-                send_sem=strip_send_sem.at[t, half],
-                recv_sem=strip_recv_sem.at[t, half],
-                device_id=(gx, there * 2 + core),
-                device_id_type=MESH,
-            )
-            for half in range(STRIPS // 8)
+            relay(sendbuf.at[there, half], recvbuf.at[chip, half], there, strip_send_sem.at[t], strip_recv_sem.at[t], half)
+            for half in range(HALVES)
         ]
 
     reach = 2 * nblocks
 
-    def pack(t, there):
+    def pack(there):
         for c in range(1, CHUNKS):
             both = jnp.concatenate(
                 [ordered[0, there, :, c * width : (c + 1) * width], got[there, :, c * width : (c + 1) * width]], axis=0
             )
             roles[:, (c - 1) * width : c * width] = permuted(deal[there], both)
-        for half, copy in enumerate(strip_sends(t, there)):
+        for half in range(HALVES):
 
             def count(role):
                 at = there * pool + half * ROLES * 8 + role * 8
@@ -640,18 +671,24 @@
                     value = jnp.where(left_n > p, left[p], right[q])
                 sendbuf[there, half, :, p * LANES : (p + 1) * LANES] = value
 
+    far = peer_of(chip, chips - 1, chips)
+    pack(far)
+    first_legs = [relay(sendbuf.at[far, half], passing.at[half], chip_x, first_leg_send_sem, first_leg_recv_sem, half) for half in range(HALVES)]
+    for copy in first_legs:
+        copy.start()
+
     def near_step(t, carry):
-        there = peer_of(chip, t + 1, chips)
-        pack(t, there)
+        pack(peer_of(chip, 2 - t, chips))
+
+        @pl.when(t == 0)
+        def _():
+            for copy in near_sends(chip_y, 1):
+                copy.start()
+
         return carry
 
-    far = peer_of(chip, chips - 1, chips)
-    pack(chips - 2, far)
-    for copy in strip_sends(chips - 2, far):
-        copy.start()
-
-
     lax.fori_loop(0, 2, near_step, 0)
+
     info_recv[gy] = info_send[chip]
     for copy in info_copies[1:]:
         copy.wait()
@@ -704,10 +741,8 @@
         copy.start()
     tails_recv[gy] = tails_send[chip]
 
-    near_copies = [strip_sends(t, peer_of(chip, t + 1, chips)) for t in range(2)]
-    for half in range(2):
-        for t in range(2):
-            near_copies[t][half].start()
+    for copy in near_sends(chip_x, 0):
+        copy.start()
 
 
     for copy in count_copies:
@@ -729,7 +764,7 @@
     )
     rcnt[...] = jnp.broadcast_to(strip_counts(got_spot_row, got_row), rcnt.shape)
     lane = lax.broadcasted_iota(jnp.int32, (total_rows, LANES), 1).astype(f32)
-    for half in range(STRIPS // 8):
+    for half in range(HALVES):
         pick = got_spot - half * ROLES * 8 == lane
         pick = jnp.where(pick & (lane < ROLES * 8), 1.0, 0.0).astype(jnp.bfloat16)
         undeal[:, half] = pick.reshape(chips, pool, LANES)
@@ -766,39 +801,25 @@
 
     lax.fori_loop(2, n_gy, first_step, 0)
 
-    def unpack(t, half):
-        there = peer_of(chip, t + 1, chips)
+    def unpack(there, t, half):
         landed = recvbuf.at[0, 0]
         pltpu.make_async_copy(landed, landed, strip_recv_sem.at[t, half]).wait()
 
-        def count(role):
-            at = there * pool + half * ROLES * 8 + role * 8
-            return rcnt[pl.ds(pl.multiple_of(at, 8), 8), :]
-
-        def block(p):
-            return recvbuf[there, half, :, p * LANES : (p + 1) * LANES]
-
-        for outer, inner, at in ((0, 1, lambda p: p), (3, 2, lambda p: STRIP_BLOCKS - 1 - p)):
-            for j in range(nblocks):
-                roles[outer * 8 : outer * 8 + 8, j * LANES : (j + 1) * LANES] = block(at(j))
-            behind = [block(at(p)) for p in range(reach)]
-            behind = shifted_down(behind, shift_bits(count(outer)), nblocks)
-            for j in range(nblocks):
-                roles[inner * 8 : inner * 8 + 8, j * LANES : (j + 1) * LANES] = behind[j]
-        order = undeal[there, half][:, : ROLES * 8]
-        for c in range(1, CHUNKS):
-            out = permuted(order, roles[: ROLES * 8, (c - 1) * width : c * width])
-            for r in range(2 * members_dev):
-                k = there * 2 * members_dev + r
-                finish_rows(k, c * width, out[r * part : (r + 1) * part], half_rows[k][:, :1] > 0.5 if half else None)
-
-    def unpack_step(t, carry):
-        for half in range(STRIPS // 8):
-            unpack(t, half)
-        return carry
-
-    for half in range(STRIPS // 8):
-        unpack(chips - 2, half)
+        def put(r, c, rows):
+            k = there * 2 * members_dev + r
+            finish_rows(k, c * width, rows, half_rows[k][:, :1] > 0.5 if half else None)
+
+        unpack_strips(recvbuf, roles, undeal, rcnt, there, half, width, part, put)
+
+    second_legs = [
+        relay(passing.at[half], recvbuf.at[chip_x, half], chip_y, strip_send_sem.at[2], strip_recv_sem.at[2], half)
+        for half in range(HALVES)
+    ]
+    for first_leg, second_leg in zip(first_legs, second_legs):
+        first_leg.wait_recv()
+        second_leg.start()
+    for half in range(HALVES):
+        unpack(chip_y, 1, half)
 
     for copy in tail_copies:
         copy.wait()
@@ -825,20 +846,71 @@
     pltpu.make_async_copy(given, given, give_send_sem.at[0]).wait()
     give_own.wait_send()
 
+    scale_ref[...] = jnp.broadcast_to(scale, scale_ref.shape)
+
+    def unpack_step(i, carry):
+        unpack(peer_of(chip, 1 + 2 * i, chips), 2 * i, 0)
+        return carry
+
     lax.fori_loop(0, 2, unpack_step, 0)
-    for t in range(chips - 1):
-        for half in range(STRIPS // 8):
+    for t in (0, 2):
+        landed = recvbuf.at[0, 0]
+        pltpu.make_async_copy(landed, landed, strip_recv_sem.at[t, 1]).wait()
+    for half in range(HALVES):
+        first_legs[half].wait_send()
+        for t in range(chips - 1):
             sent = sendbuf.at[0, 0]
             pltpu.make_async_copy(sent, sent, strip_send_sem.at[t, half]).wait()
 
 
-def store(done, loss, adv, grad, loss_out, adv_out, sem):
-    copies = [
-        pltpu.make_async_copy(src, dst, sem.at[k])
-        for k, (src, dst) in enumerate(((done, grad), (loss, loss_out), (adv, adv_out)))
+def store(
+    n_gy, done, loss, adv, recvbuf, undeal, rcnt, len_rows, adv_rows, half_rows, scale_ref,
+    grad, loss_out, adv_out, last, roles, sem,
+):
+    chips = n_gy // 2
+    members, part, seq = done.shape
+    group = members // chips
+    width = seq - roles.shape[1]
+    chip = lax.axis_index("gy") // 2
+    scale = scale_ref[:1, :1]
+    lane_width = lax.broadcasted_iota(jnp.int32, (part, width), 1).astype(jnp.float32)
+
+    def chip_rows(there):
+        return pl.ds(there * group, group)
+
+    whole = [chip_rows(chip), chip_rows(peer_of(chip, 2, chips))]
+    late = [peer_of(chip, 1, chips), peer_of(chip, 3, chips)]
+    first = pl.ds(0, width)
+    copies = [pltpu.make_async_copy(done.at[rows], grad.at[rows], sem.at[k]) for k, rows in enumerate(whole)]
+    copies += [
+        pltpu.make_async_copy(done.at[chip_rows(there), :, first], grad.at[chip_rows(there), :, first], sem.at[2 + k])
+        for k, there in enumerate(late)
     ]
+    copies += [pltpu.make_async_copy(loss, loss_out, sem.at[4]), pltpu.make_async_copy(adv, adv_out, sem.at[5])]
     for copy in copies:
         copy.start()
+
+    def store_late(i):
+        rows = chip_rows(peer_of(chip, 1 + 2 * i, chips))
+        return pltpu.make_async_copy(last.at[i], grad.at[rows, :, pl.ds(width, seq - width)], sem.at[6 + i])
+
+    def late_step(i, carry):
+        there = peer_of(chip, 1 + 2 * i, chips)
+
+        def put(r, c, rows):
+            k = there * group + r
+            value = (rows - adv_rows[k][:, :1]) * scale
+            valid = lane_width < len_rows[k][:, :1] - c * width
+            before = done[k, :, c * width : (c + 1) * width]
+            value = jnp.where(half_rows[k][:, :1] > 0.5, jnp.where(valid, value, 0.0), before)
+            last[i, r, :, (c - 1) * width : c * width] = value
+
+        unpack_strips(recvbuf, roles, undeal, rcnt, there, 1, width, part, put)
+        store_late(i).start()
+        return carry
+
+    lax.fori_loop(0, 2, late_step, 0)
+    copies += [store_late(i) for i in range(2)]
     for copy in copies:
         copy.wait()
 
@@ -851,23 +923,32 @@
     pool = 2 * rows
     width = seq // CHUNKS
     chunked = (CHUNKS, members_dev, slots, width)
-    strips = (chips, STRIPS // 8, 8, STRIP_BLOCKS * LANES)
+    strips = (chips, HALVES, 8, STRIP_BLOCKS * LANES)
     per_slot = (members_dev, slots, LANES)
     per_sample = (members, part, LANES)
     tile = (n_gy, 8, LANES)
     hbm_spec = pl.BlockSpec(memory_space=pltpu.HBM)
     vmem_spec = pl.BlockSpec(memory_space=pltpu.VMEM)
     dma = pltpu.SemaphoreType.DMA
-    done, loss, adv, over = pl.pallas_call(
+    handed = (
+        pltpu.VMEM(strips, f32),
+        pltpu.VMEM((chips, HALVES, pool, LANES), bf16),
+        pltpu.VMEM((chips * pool, LANES), f32),
+        pltpu.VMEM(per_sample, f32),
+        pltpu.VMEM(per_sample, f32),
+        pltpu.VMEM(per_sample, f32),
+        pltpu.VMEM((8, LANES), f32),
+    )
+    done, loss, adv, over, *rest = pl.pallas_call(
         functools.partial(packed_exchange, n_gx, n_gy),
         out_shape=(
             pltpu.VMEM((members, part, seq), f32),
             pltpu.VMEM((members, part), f32),
             pltpu.VMEM((members, part), f32),
             pltpu.SMEM((1, 1), jnp.int32),
-        ),
+        ) + handed,
         in_specs=[hbm_spec] * 5,
-        out_specs=(vmem_spec,) * 3 + (pl.BlockSpec(memory_space=pltpu.SMEM),),
+        out_specs=(vmem_spec,) * 3 + (pl.BlockSpec(memory_space=pltpu.SMEM),) + (vmem_spec,) * len(handed),
         scratch_shapes=[
             pltpu.VMEM(chunked, f32),
             pltpu.VMEM(chunked, f32),
@@ -879,18 +960,13 @@
             pltpu.VMEM((chips, rows, seq), f32),
             pltpu.VMEM((n_gy, rows, width), f32),
             pltpu.VMEM(strips, f32),
-            pltpu.VMEM(strips, f32),
+            pltpu.VMEM(strips[1:], f32),
             pltpu.VMEM((pool, seq - width), f32),
             pltpu.VMEM((chips, pool, pool), bf16),
-            pltpu.VMEM((chips, STRIPS // 8, pool, LANES), bf16),
-            pltpu.VMEM((chips * pool, LANES), f32),
             pltpu.VMEM((chips * pool, LANES), f32),
             pltpu.VMEM(per_slot, f32),
             pltpu.VMEM(per_slot, f32),
             pltpu.VMEM(per_slot, f32),
-            pltpu.VMEM(per_sample, f32),
-            pltpu.VMEM(per_sample, f32),
-            pltpu.VMEM(per_sample, f32),
             pltpu.VMEM(tile, f32),
             pltpu.VMEM((chips, 8, LANES), f32),
             pltpu.VMEM(tile, f32),
@@ -904,8 +980,10 @@
             dma((2,)),
             dma((n_gy - 2,)),
             dma((n_gy - 2,)),
-            dma((chips - 1, STRIPS // 8)),
-            dma((chips - 1, STRIPS // 8)),
+            dma((chips - 1, HALVES)),
+            dma((chips - 1, HALVES)),
+            dma((HALVES,)),
+            dma((HALVES,)),
             dma((n_gy - 1,)),
             dma((n_gy - 1,)),
             dma((n_gy - 1,)),
@@ -915,26 +993,30 @@
             dma((n_gx - 1,)),
             dma((n_gx - 1,)),
         ],
-        compiler_params=pltpu.CompilerParams(collective_id=0, has_side_effects=True, vmem_limit_bytes=56 * 2**20),
+        compiler_params=pltpu.CompilerParams(collective_id=0, has_side_effects=True, vmem_limit_bytes=36 * 2**20),
     )(policy_logp, anchor_logp, lengths, rewards, slot_prompt)
 
-    def fits(policy_logp, anchor_logp, lengths, rewards, slot_prompt, done, loss, adv):
+    def fits(policy_logp, anchor_logp, lengths, rewards, slot_prompt, done, loss, adv, *rest):
         small = jax.ShapeDtypeStruct((members, part), f32)
         return tuple(pl.pallas_call(
-            store,
+            functools.partial(store, n_gy),
             out_shape=(jax.ShapeDtypeStruct((members, part, seq), f32), small, small),
-            in_specs=[vmem_spec] * 3,
+            in_specs=[vmem_spec] * (3 + len(rest)),
             out_specs=(hbm_spec,) * 3,
-            scratch_shapes=[dma((3,))],
+            scratch_shapes=[
+                pltpu.VMEM((2, 2 * members_dev, part, seq - width), f32),
+                pltpu.VMEM((ROLES * 8, seq - width), f32),
+                dma((8,)),
+            ],
             compiler_params=pltpu.CompilerParams(vmem_limit_bytes=16 * 2**20),
-        )(done, loss, adv))
-
-    def overflows(policy_logp, anchor_logp, lengths, rewards, slot_prompt, done, loss, adv):
+        )(done, loss, adv, *rest))
+
+    def overflows(policy_logp, anchor_logp, lengths, rewards, slot_prompt, done, loss, adv, *rest):
         return tuple(unpacked_body(n_gx, n_gy, policy_logp, anchor_logp, lengths, rewards, slot_prompt))
 
     return lax.cond(
         over[0, 0] > 0, overflows, fits,
-        policy_logp, anchor_logp, lengths, rewards, slot_prompt, done, loss, adv,
+        policy_logp, anchor_logp, lengths, rewards, slot_prompt, done, loss, adv, *rest,
     )
 
 

time: 44.6 us -> 44 us (0.987)
  Pallas kernels: 43.7 us -> 43.1 us
    pallas_call x1, Pallas kernels: 41.7 us -> 41 us  [packed_body(): pl.pallas_call(functools.partial(packed_exchange, n_gx, n_gy), out_shape=...]
where the time goes in v2:
time: 44 us; the launch traced here: 43.9 us
  Pallas kernels  43.1 us (98%)
  between operations  0.69 us (2%)
    pallas_call x1, Pallas kernels, packed_body(): pl.pallas_call(functools.partial(packed_exchange, n_gx, n_gy), out_shape=...  41 us
    pallas_call x1, Pallas kernels, fits(): pl.pallas_call(functools.partial(store, n_gy), out_shape=(jax.ShapeDtypeS...  2.17 us

profile of v2, /device:TPU:0, one launch (start us, length us, event | category | flops | bytes accessed | tf_op | source)
XLA Modules:
  0.0 43.9 jit_solution(9690330206679216481)
XLA Ops:
  0.6 0.0 copy-start
  0.6 0.0 copy-start.1
  0.7 0.0 copy-start.2
  0.7 41.0 %shard_map.82 = (f32[16,16,4096]{2,1,0:T(8,128)S(1)}, f32[16,16]{1,0:T(8,128)S(1)}, f32[16,16]{1,0:T(8,128)S(1)}, s32[1,1]{1,0:T(1,128)S(4)}, f32[4,2,8,9472]{3,...) custom-call(f32[2,128,4096]{2,1,0:T(8,128)} %policy_hbm.1, ...), custom_call_target="tpu_custom_call" | custom-call | tf_op jit(solution)/shard_map/pallas_call | solution.py:942
  41.6 0.0 copy-done
  41.7 0.0 copy-done.1
  41.7 0.0 copy-done.2
  41.7 2.2 %conditional.1 = ((f32[16,16,4096]{2,1,0:T(8,128)}, f32[16,16]{1,0:T(8,128)}, f32[16,16]{1,0:T(8,128)})) conditional(s32[]{:T(128)} %bitcast, (f32[16,16,4096]{2,1,0:T(8,128)S(1)}, f32[16,16]{1,0:T(8,128)S(1)}, f32[16,16]{1,0:T(8,128)S(1)}, f32[4,2,8,9472]{3,2,1,0:T(8,128)S(1)}, bf16[4,2,64,128]{3,2,1,0:T(8,128)(2,1)S(1)}, ...), branch_computations={%region_0.0_spmd, %region_1.0_spmd} | conditional | bytes 8 | solution.py:1017
  41.7 2.2 %branch_0_fun.1 = (f32[16,16,4096]{2,1,0:T(8,128)}, f32[16,16]{1,0:T(8,128)}, f32[16,16]{1,0:T(8,128)}) custom-call(f32[16,16,4096]{2,1,0:T(8,128)S(1)} %get-tuple-element.30.done, f32[16,16]{1,0:T(8,128)S(1)} %get-tuple-element.31.loss, f32[16,16]{1,0:T(8,128)S(1)} %get-tuple-element.32.adv, f32[4,2,8,9472]{3,2,1,0:T(8,128)S(1)} %get-tuple-element.33.recvbuf, ...), custom_call_target="tpu_custom_call" | custom-call | tf_op jit(solution)/shard_map/cond/branch_0_fun/pallas_call | solution.py:1001
Async XLA Ops:
  0.6 41.0 %copy-start = (s32[2,128]{1,0:T(2,128)S(1)}, s32[2,128]{1,0:T(2,128)}, u32[]{:S(2)}) copy-start(s32[2,128]{1,0:T(2,128)} %len_hbm.1) | copy-start | bytes 3076
  0.6 41.0 %copy-start.1 = (s32[2,128]{1,0:T(2,128)S(1)}, s32[2,128]{1,0:T(2,128)}, u32[]{:S(2)}) copy-start(s32[2,128]{1,0:T(2,128)} %reward_hbm.1) | copy-start | bytes 3076
  0.7 41.0 %copy-start.2 = (s32[2,128]{1,0:T(2,128)S(1)}, s32[2,128]{1,0:T(2,128)}, u32[]{:S(2)}) copy-start(s32[2,128]{1,0:T(2,128)} %prompt_hbm.1) | copy-start | bytes 3076

commit v3 on v2

--- a/solution.py
+++ b/solution.py
@@ -15,8 +15,11 @@
 STRIPS = 16
 HALVES = STRIPS // 8
 SHIFTS = 5
-HEAD_BLOCKS = 4
-STRIP_BLOCKS = 74
+PIECES = 8
+DEALS = 1
+UNDEALS = 1
+HEAD_BLOCKS = 6
+STRIP_BLOCKS = 66
 FIRST_ORDER = (2, 4, 3, 5, 6, 7)
 
 
@@ -352,7 +355,7 @@
 
 
 def tail_blocks(lens):
-    return jnp.floor((lens + (LANES - 1)) * (1.0 / LANES)) - HEAD_BLOCKS
+    return jnp.maximum(jnp.floor((lens + (LANES - 1)) * (1.0 / LANES)) - HEAD_BLOCKS, 0.0)
 
 
 def shift_bits(count):
@@ -394,7 +397,7 @@
     return out
 
 
-def unpack_strips(recvbuf, roles, undeal, rcnt, there, half, width, part, put):
+def unpack_strips(recvbuf, roles, undeal, rcnt, there, half, part, put):
     pool, seq_tail = undeal.shape[2], roles.shape[1]
     nblocks = seq_tail // LANES
 
@@ -413,10 +416,16 @@
         for j in range(nblocks):
             roles[inner * 8 : inner * 8 + 8, j * LANES : (j + 1) * LANES] = behind[j]
     order = undeal[there, half][:, : ROLES * 8]
-    for c in range(seq_tail // width):
-        out = permuted(order, roles[: ROLES * 8, c * width : (c + 1) * width])
+    span = seq_tail // UNDEALS
+
+    def undeal_step(i, carry):
+        start = pl.multiple_of(i * span, LANES)
+        out = permuted(order, roles[: ROLES * 8, pl.ds(start, span)])
         for r in range(pool // part):
-            put(r, c + 1, out[r * part : (r + 1) * part])
+            put(r, start, out[r * part : (r + 1) * part])
+        return carry
+
+    lax.fori_loop(0, UNDEALS, undeal_step, 0)
 
 
 def packed_exchange(
@@ -434,7 +443,8 @@
     members_dev, slots, seq = policy_hbm.shape
     members, part = members_dev * n_gy, slots // n_gy
     chips = n_gy // 2
-    width = seq // CHUNKS
+    width = HEAD_BLOCKS * LANES
+    piece = seq // PIECES
     nblocks = seq // LANES - HEAD_BLOCKS
     rows = members_dev * part
     pool = 2 * rows
@@ -451,7 +461,7 @@
         copy.start()
 
     def loads(c):
-        cols = pl.ds(pl.multiple_of(c * width, LANES), width)
+        cols = pl.ds(pl.multiple_of(c * piece, LANES), piece)
         return (
             pltpu.make_async_copy(policy_hbm.at[:, :, cols], policy.at[c], load_sem.at[0, c]),
             pltpu.make_async_copy(anchor_hbm.at[:, :, cols], anchor.at[c], load_sem.at[1, c]),
@@ -464,7 +474,7 @@
         pl.semaphore_signal(barrier, inc=1, device_id=(gx, partner(gy, off, n_gy)), device_id_type=MESH)
     for off in range(1, n_gx):
         pl.semaphore_signal(barrier, inc=1, device_id=(lax.rem(gx + off, n_gx), gy), device_id_type=MESH)
-    for c in range(1, CHUNKS):
+    for c in range(1, PIECES):
         for copy in loads(c):
             copy.start()
     for copy in small_loads:
@@ -486,12 +496,12 @@
         for copy in loads(c):
             copy.wait()
         values = kl_weight * (1.0 - jnp.exp(anchor[c] - policy[c]))
-        out = permuted(onehot[...], values.reshape(members_dev * slots, width))
-        cols = pl.ds(pl.multiple_of(c * width, LANES), width)
-        ordered[:, :, :, cols] = out.reshape(2, chips, rows, width)
+        out = permuted(onehot[...], values.reshape(members_dev * slots, piece))
+        cols = pl.ds(pl.multiple_of(c * piece, LANES), piece)
+        ordered[:, :, :, cols] = out.reshape(2, chips, rows, piece)
 
     def give(c, there):
-        cols = pl.ds(pl.multiple_of(c * width, LANES), width)
+        cols = pl.ds(pl.multiple_of(c * piece, LANES), piece)
         return pltpu.make_async_remote_copy(
             src_ref=ordered.at[1, there, :, cols],
             dst_ref=got.at[there, :, cols],
@@ -509,24 +519,19 @@
         device_id=(gx, mate),
         device_id_type=MESH,
     )
-    given = got.at[pl.ds(0, chips - 1), :, pl.ds(width, seq - width)]
-
-    def first_send(off):
+    given = got.at[pl.ds(0, chips - 1), :, pl.ds(piece, seq - piece)]
+
+    def first_send(off, lo, hi):
         peer = partner(gy, off, n_gy)
+        cols = pl.ds(lo, hi - lo)
         return pltpu.make_async_remote_copy(
-            src_ref=ordered.at[off % 2, peer // 2, :, pl.ds(0, width)],
-            dst_ref=heads_in.at[gy],
+            src_ref=ordered.at[off % 2, peer // 2, :, cols],
+            dst_ref=heads_in.at[gy, :, cols],
             send_sem=first_send_sem.at[off - 2],
             recv_sem=first_recv_sem.at[off - 2],
             device_id=(gx, peer),
             device_id_type=MESH,
         )
-
-    put_in_order(0)
-    pl.semaphore_wait(barrier, n_gy - 1 + n_gx - 1)
-    first_copies = [first_send(off) for off in FIRST_ORDER]
-    for copy in first_copies:
-        copy.start()
 
     tile_lane = lax.broadcasted_iota(jnp.int32, (n_gy, 8, LANES), 2)
     groups = rows // 8
@@ -543,11 +548,6 @@
     def column_in(tile, f):
         parts = [tile[:, :, g * 4 + f : g * 4 + f + 1][:, None] for g in range(groups)]
         return jnp.concatenate(parts, axis=1)
-
-    own_len = row_sums(place, targets, lens)
-    rewards = [reward_ref[m : m + 1, :].astype(f32) * 0.25 for m in range(members_dev)]
-    own_reward = row_sums(place, targets, rewards)
-    info_send[...] = tiles((own_len, own_reward), jnp.broadcast_to(local_tokens, (n_gy, 8, LANES)))
 
     def tile_sends(src, dst, send, recv, offs):
         copies = []
@@ -574,17 +574,37 @@
         device_id_type=MESH,
     )
     info_copies = [mate_info] + tile_sends(info_send, info_recv, info_send_sem, info_recv_sem, range(2, n_gy))
-    for copy in info_copies:
-        copy.start()
 
     def order_step(c, carry):
         put_in_order(c)
-        for t in range(1, chips):
-            give(c, peer_of(chip, t, chips)).start()
+
+        @pl.when(c == 0)
+        def _():
+            pl.semaphore_wait(barrier, n_gy - 1 + n_gx - 1)
+            for off in FIRST_ORDER:
+                first_send(off, 0, piece).start()
+            lens_out = row_sums(place, targets, lens)
+            rewards = [reward_ref[m : m + 1, :].astype(f32) * 0.25 for m in range(members_dev)]
+            rewards_out = row_sums(place, targets, rewards)
+            info_send[...] = tiles((lens_out, rewards_out), jnp.broadcast_to(local_tokens, (n_gy, 8, LANES)))
+            for copy in info_copies:
+                copy.start()
+
+        @pl.when(c == 1)
+        def _():
+            for off in FIRST_ORDER:
+                first_send(off, piece, width).start()
+
+        @pl.when(c >= 1)
+        def _():
+            for t in range(1, chips):
+                give(c, peer_of(chip, t, chips)).start()
+
         return carry
 
-    lax.fori_loop(1, CHUNKS, order_step, 0)
+    lax.fori_loop(0, PIECES, order_step, 0)
     give_own.start()
+    own_len = column_in(info_send[:chips], 0).reshape(chips * rows, 1)
 
     mate_info.wait()
     pair_lens = jnp.concatenate(
@@ -638,20 +658,24 @@
     reach = 2 * nblocks
 
     def pack(there):
-        for c in range(1, CHUNKS):
-            both = jnp.concatenate(
-                [ordered[0, there, :, c * width : (c + 1) * width], got[there, :, c * width : (c + 1) * width]], axis=0
-            )
-            roles[:, (c - 1) * width : c * width] = permuted(deal[there], both)
-        for half in range(HALVES):
-
+        span = (seq - width) // DEALS
+
+        def deal_step(i, carry):
+            cols = pl.ds(pl.multiple_of(width + i * span, LANES), span)
+            both = jnp.concatenate([ordered[0, there, :, cols], got[there, :, cols]], axis=0)
+            roles[:, pl.ds(pl.multiple_of(i * span, LANES), span)] = permuted(deal[there], both)
+            return carry
+
+        lax.fori_loop(0, DEALS, deal_step, 0)
+
+        def half_step(half, carry):
             def count(role):
                 at = there * pool + half * ROLES * 8 + role * 8
                 return cnt[pl.ds(pl.multiple_of(at, 8), 8), :]
 
             def blocks(role):
-                at = half * ROLES * 8 + role * 8
-                return [roles[at : at + 8, j * LANES : (j + 1) * LANES] for j in range(nblocks)]
+                at = pl.ds(pl.multiple_of(half * ROLES * 8 + role * 8, 8), 8)
+                return [roles[at, j * LANES : (j + 1) * LANES] for j in range(nblocks)]
 
             def side(outer, inner):
                 n = count(outer)
@@ -670,24 +694,29 @@
                 else:
                     value = jnp.where(left_n > p, left[p], right[q])
                 sendbuf[there, half, :, p * LANES : (p + 1) * LANES] = value
+            return carry
+
+        lax.fori_loop(0, HALVES, half_step, 0)
 
     far = peer_of(chip, chips - 1, chips)
-    pack(far)
     first_legs = [relay(sendbuf.at[far, half], passing.at[half], chip_x, first_leg_send_sem, first_leg_recv_sem, half) for half in range(HALVES)]
-    for copy in first_legs:
-        copy.start()
-
-    def near_step(t, carry):
-        pack(peer_of(chip, 2 - t, chips))
+
+    def pack_step(t, carry):
+        pack(peer_of(chip, chips - 1 - t, chips))
 
         @pl.when(t == 0)
+        def _():
+            for copy in first_legs:
+                copy.start()
+
+        @pl.when(t == 1)
         def _():
             for copy in near_sends(chip_y, 1):
                 copy.start()
 
         return carry
 
-    lax.fori_loop(0, 2, near_step, 0)
+    lax.fori_loop(0, chips - 1, pack_step, 0)
 
     info_recv[gy] = info_send[chip]
     for copy in info_copies[1:]:
@@ -720,7 +749,7 @@
     sum_kl[...] = jnp.zeros_like(sum_kl)
 
     def sum_step(c, carry):
-        positions = (lax.broadcasted_iota(jnp.int32, (slots, width), 1) + c * width).astype(f32)
+        positions = (lax.broadcasted_iota(jnp.int32, (slots, piece), 1) + c * piece).astype(f32)
         for m in range(members_dev):
             pol = policy[c, m]
             log_ratio = anchor[c, m] - pol
@@ -730,7 +759,7 @@
             sum_kl[m] += folded(jnp.where(valid, kl_weight * (ratio - log_ratio - 1.0), 0.0))
         return carry
 
-    lax.fori_loop(0, CHUNKS, sum_step, 0)
+    lax.fori_loop(0, PIECES, sum_step, 0)
     sums = []
     for buf in (sum_policy, sum_kl):
         per_member = [row_of(jnp.sum(buf[m], axis=1, keepdims=True)) for m in range(members_dev)]
@@ -769,24 +798,28 @@
         pick = jnp.where(pick & (lane < ROLES * 8), 1.0, 0.0).astype(jnp.bfloat16)
         undeal[:, half] = pick.reshape(chips, pool, LANES)
     half_rows[...] = jnp.broadcast_to(jnp.where(got_spot < ROLES * 8, 0.0, 1.0).reshape(members, part, 1), half_rows.shape)
-    lane_width = lax.broadcasted_iota(jnp.int32, (part, width), 1).astype(f32)
-
     def finish_rows(k, start, value, only=None):
+        span = value.shape[1]
+        cols = pl.ds(pl.multiple_of(start, LANES), span)
+        positions = (lax.broadcasted_iota(jnp.int32, (part, span), 1) + start).astype(f32)
         value = (value - adv_rows[k][:, :1]) * scale
-        valid = lane_width < len_rows[k][:, :1] - start
-        value = jnp.where(valid, value, 0.0)
+        value = jnp.where(positions < len_rows[k][:, :1], value, 0.0)
         if only is not None:
-            value = jnp.where(only, value, done[k, :, start : start + width])
-        done[k, :, start : start + width] = value
+            value = jnp.where(only, value, done[k, :, cols])
+        done[k, :, cols] = value
 
     def own_step(which, source):
-        for m in range(members_dev):
-            for c in range(CHUNKS):
-                finish_rows(source * members_dev + m, c * width, which(m * part, c * width))
-
-    own_step(lambda r, s: ordered[0, chip, r : r + part, s : s + width], gy)
+        def column_step(c, carry):
+            start = pl.multiple_of(c * piece, LANES)
+            for m in range(members_dev):
+                finish_rows(source * members_dev + m, start, which(m * part, pl.ds(start, piece)))
+            return carry
+
+        lax.fori_loop(0, PIECES, column_step, 0)
+
+    own_step(lambda r, cols: ordered[0, chip, r : r + part, cols], gy)
     give_own.wait_recv()
-    own_step(lambda r, s: got[chip, r : r + part, s : s + width], mate)
+    own_step(lambda r, cols: got[chip, r : r + part, cols], mate)
 
     def first_wait(off):
         landed = heads_in.at[0]
@@ -805,11 +838,11 @@
         landed = recvbuf.at[0, 0]
         pltpu.make_async_copy(landed, landed, strip_recv_sem.at[t, half]).wait()
 
-        def put(r, c, rows):
+        def put(r, start, rows):
             k = there * 2 * members_dev + r
-            finish_rows(k, c * width, rows, half_rows[k][:, :1] > 0.5 if half else None)
-
-        unpack_strips(recvbuf, roles, undeal, rcnt, there, half, width, part, put)
+            finish_rows(k, width + start, rows, half_rows[k][:, :1] > 0.5 if half else None)
+
+        unpack_strips(recvbuf, roles, undeal, rcnt, there, half, part, put)
 
     second_legs = [
         relay(passing.at[half], recvbuf.at[chip_x, half], chip_y, strip_send_sem.at[2], strip_recv_sem.at[2], half)
@@ -841,8 +874,9 @@
     for off in range(1, n_gx):
         fullest = jnp.maximum(fullest, needs[off])
     over_ref[0, 0] = (jnp.max(fullest[:, fill_lane : fill_lane + 1]) > STRIP_BLOCKS).astype(jnp.int32)
-    for copy in first_copies:
-        copy.wait_send()
+    for off in FIRST_ORDER:
+        landed = heads_in.at[0]
+        pltpu.make_async_copy(landed, landed, first_send_sem.at[off - 2]).wait()
     pltpu.make_async_copy(given, given, give_send_sem.at[0]).wait()
     give_own.wait_send()
 
@@ -873,7 +907,6 @@
     width = seq - roles.shape[1]
     chip = lax.axis_index("gy") // 2
     scale = scale_ref[:1, :1]
-    lane_width = lax.broadcasted_iota(jnp.int32, (part, width), 1).astype(jnp.float32)
 
     def chip_rows(there):
         return pl.ds(there * group, group)
@@ -897,15 +930,15 @@
     def late_step(i, carry):
         there = peer_of(chip, 1 + 2 * i, chips)
 
-        def put(r, c, rows):
-            k = there * group + r
+        def put(r, start, rows):
+            k, span = there * group + r, rows.shape[1]
+            positions = (lax.broadcasted_iota(jnp.int32, (part, span), 1) + (width + start)).astype(jnp.float32)
             value = (rows - adv_rows[k][:, :1]) * scale
-            valid = lane_width < len_rows[k][:, :1] - c * width
-            before = done[k, :, c * width : (c + 1) * width]
-            value = jnp.where(half_rows[k][:, :1] > 0.5, jnp.where(valid, value, 0.0), before)
-            last[i, r, :, (c - 1) * width : c * width] = value
-
-        unpack_strips(recvbuf, roles, undeal, rcnt, there, 1, width, part, put)
+            before = done[k, :, pl.ds(pl.multiple_of(width + start, LANES), span)]
+            value = jnp.where(half_rows[k][:, :1] > 0.5, jnp.where(positions < len_rows[k][:, :1], value, 0.0), before)
+            last[i, r, :, pl.ds(start, span)] = value
+
+        unpack_strips(recvbuf, roles, undeal, rcnt, there, 1, part, put)
         store_late(i).start()
         return carry
 
@@ -921,8 +954,8 @@
     f32, bf16 = jnp.float32, jnp.bfloat16
     chips, rows = n_gy // 2, members_dev * part
     pool = 2 * rows
-    width = seq // CHUNKS
-    chunked = (CHUNKS, members_dev, slots, width)
+    width = HEAD_BLOCKS * LANES
+    chunked = (PIECES, members_dev, slots, seq // PIECES)
     strips = (chips, HALVES, 8, STRIP_BLOCKS * LANES)
     per_slot = (members_dev, slots, LANES)
     per_sample = (members, part, LANES)
@@ -975,7 +1008,7 @@
             pltpu.VMEM((n_gx, 8, LANES), f32),
             pltpu.VMEM((n_gx, 8, LANES), f32),
             dma((3,)),
-            dma((2, CHUNKS)),
+            dma((2, PIECES)),
             dma((2,)),
             dma((2,)),
             dma((n_gy - 2,)),
@@ -1023,7 +1056,7 @@
 def body(n_gx, n_gy, *args):
     members_dev, slots, seq = args[0].shape
     pool = 2 * members_dev * slots // n_gy
-    packs = n_gy == 8 and pool == ROLES * STRIPS and slots == LANES and seq == LANES * 32 and seq == CHUNKS * HEAD_BLOCKS * LANES
+    packs = n_gy == 8 and pool == ROLES * STRIPS and slots == LANES and seq == LANES * 32 and seq % (PIECES * LANES) == 0
     return (packed_body if packs else unpacked_body)(n_gx, n_gy, *args)
 
 

time: 44 us -> 43.4 us (0.986)
  Pallas kernels: 43.1 us -> 42.5 us
    pallas_call x1, Pallas kernels: 41 us -> 40.3 us  [packed_body(): pl.pallas_call(functools.partial(packed_exchange, n_gx, n_gy), out_shape=...]
where the time goes in v3:
time: 43.4 us; the launch traced here: 43.2 us
  Pallas kernels  42.5 us (98%)
  between operations  0.69 us (2%)
    pallas_call x1, Pallas kernels, packed_body(): pl.pallas_call(functools.partial(packed_exchange, n_gx, n_gy), out_shape=...  40.3 us
    pallas_call x1, Pallas kernels, fits(): pl.pallas_call(functools.partial(store, n_gy), out_shape=(jax.ShapeDtypeS...  2.16 us

profile of v3, /device:TPU:0, one launch (start us, length us, event | category | flops | bytes accessed | tf_op | source)
XLA Modules:
  0.0 43.2 jit_solution(7736524114896639358)
XLA Ops:
  0.6 0.0 copy-start
  0.6 0.0 copy-start.1
  0.7 0.0 copy-start.2
  0.7 40.3 %shard_map.82 = (f32[16,16,4096]{2,1,0:T(8,128)S(1)}, f32[16,16]{1,0:T(8,128)S(1)}, f32[16,16]{1,0:T(8,128)S(1)}, s32[1,1]{1,0:T(1,128)S(4)}, f32[4,2,8,8448]{3,...) custom-call(f32[2,128,4096]{2,1,0:T(8,128)} %policy_hbm.1, ...), custom_call_target="tpu_custom_call" | custom-call | tf_op jit(solution)/shard_map/pallas_call | solution.py:975
  41.0 0.0 copy-done
  41.0 0.0 copy-done.1
  41.0 0.0 copy-done.2
  41.0 2.2 %conditional.1 = ((f32[16,16,4096]{2,1,0:T(8,128)}, f32[16,16]{1,0:T(8,128)}, f32[16,16]{1,0:T(8,128)})) conditional(s32[]{:T(128)} %bitcast, (f32[16,16,4096]{2,1,0:T(8,128)S(1)}, f32[16,16]{1,0:T(8,128)S(1)}, f32[16,16]{1,0:T(8,128)S(1)}, f32[4,2,8,8448]{3,2,1,0:T(8,128)S(1)}, bf16[4,2,64,128]{3,2,1,0:T(8,128)(2,1)S(1)}, ...), branch_computations={%region_0.0_spmd, %region_1.0_spmd} | conditional | bytes 8 | solution.py:1050
  41.1 2.2 %branch_0_fun.1 = (f32[16,16,4096]{2,1,0:T(8,128)}, f32[16,16]{1,0:T(8,128)}, f32[16,16]{1,0:T(8,128)}) custom-call(f32[16,16,4096]{2,1,0:T(8,128)S(1)} %get-tuple-element.30.done, f32[16,16]{1,0:T(8,128)S(1)} %get-tuple-element.31.loss, f32[16,16]{1,0:T(8,128)S(1)} %get-tuple-element.32.adv, f32[4,2,8,8448]{3,2,1,0:T(8,128)S(1)} %get-tuple-element.33.recvbuf, ...), custom_call_target="tpu_custom_call" | custom-call | tf_op jit(solution)/shard_map/cond/branch_0_fun/pallas_call | solution.py:1034
Async XLA Ops:
  0.6 40.4 %copy-start = (s32[2,128]{1,0:T(2,128)S(1)}, s32[2,128]{1,0:T(2,128)}, u32[]{:S(2)}) copy-start(s32[2,128]{1,0:T(2,128)} %len_hbm.1) | copy-start | bytes 3076
  0.6 40.4 %copy-start.1 = (s32[2,128]{1,0:T(2,128)S(1)}, s32[2,128]{1,0:T(2,128)}, u32[]{:S(2)}) copy-start(s32[2,128]{1,0:T(2,128)} %reward_hbm.1) | copy-start | bytes 3076
  0.7 40.4 %copy-start.2 = (s32[2,128]{1,0:T(2,128)S(1)}, s32[2,128]{1,0:T(2,128)}, u32[]{:S(2)}) copy-start(s32[2,128]{1,0:T(2,128)} %prompt_hbm.1) | copy-start | bytes 3076

commit v4 on v3

--- a/solution.py
+++ b/solution.py
@@ -433,9 +433,9 @@
     done, loss_ref, adv_ref, over_ref, recvbuf, undeal, rcnt, len_rows, adv_rows, half_rows, scale_ref,
     policy, anchor, len_ref, reward_ref, prompt_ref, onehot, ordered, got, heads_in, sendbuf, passing, roles,
     deal, cnt, len_col, sum_policy, sum_kl,
-    info_send, info_got, info_recv, tails_send, tails_recv, counts, needs,
+    info_send, info_got, info_recv, tails_send, tails_recv, counts,
     small_sem, load_sem, give_send_sem, give_recv_sem, first_send_sem, first_recv_sem, strip_send_sem, strip_recv_sem, first_leg_send_sem, first_leg_recv_sem,
-    info_send_sem, info_recv_sem, tail_send_sem, tail_recv_sem, count_send_sem, count_recv_sem, need_send_sem, need_recv_sem,
+    info_send_sem, info_recv_sem, tail_send_sem, tail_recv_sem, count_send_sem, count_recv_sem,
 ):
     gx, gy = lax.axis_index("gx"), lax.axis_index("gy")
     core, chip = lax.rem(gy, 2), gy // 2
@@ -451,6 +451,7 @@
     total_rows = chips * pool
     samples = members * slots * n_gx
     info_lane, fill_lane = 16, 17
+    rounds = n_gx.bit_length() - 1
     f32 = jnp.float32
 
     small_loads = [
@@ -472,8 +473,8 @@
     barrier = pltpu.get_barrier_semaphore()
     for off in range(1, n_gy):
         pl.semaphore_signal(barrier, inc=1, device_id=(gx, partner(gy, off, n_gy)), device_id_type=MESH)
-    for off in range(1, n_gx):
-        pl.semaphore_signal(barrier, inc=1, device_id=(lax.rem(gx + off, n_gx), gy), device_id_type=MESH)
+    for k in range(rounds):
+        pl.semaphore_signal(barrier, inc=1, device_id=(partner(gx, 2**k, n_gx), gy), device_id_type=MESH)
     for c in range(1, PIECES):
         for copy in loads(c):
             copy.start()
@@ -580,7 +581,7 @@
 
         @pl.when(c == 0)
         def _():
-            pl.semaphore_wait(barrier, n_gy - 1 + n_gx - 1)
+            pl.semaphore_wait(barrier, n_gy - 1 + rounds)
             for off in FIRST_ORDER:
                 first_send(off, 0, piece).start()
             lens_out = row_sums(place, targets, lens)
@@ -723,24 +724,25 @@
         copy.wait()
     info_recv[mate] = info_got[chip]
     arrived = info_recv[...]
-    counts[0] = jnp.sum(arrived, axis=0)
-
-    def axis_sends(buf, send, recv):
-        return [
-            pltpu.make_async_remote_copy(
-                src_ref=buf.at[0],
-                dst_ref=buf.at[off],
-                send_sem=send.at[off - 1],
-                recv_sem=recv.at[off - 1],
-                device_id=(lax.rem(gx + off, n_gx), gy),
-                device_id_type=MESH,
-            )
-            for off in range(1, n_gx)
-        ]
-
-    count_copies = axis_sends(counts, count_send_sem, count_recv_sem)
-    for copy in count_copies:
-        copy.start()
+    fill_here = lax.broadcasted_iota(jnp.int32, (8, LANES), 1) == fill_lane
+    counts[0] = jnp.where(fill_here, local_fill, jnp.sum(arrived, axis=0))
+
+    def count_send(k):
+        return pltpu.make_async_remote_copy(
+            src_ref=counts.at[2 * k],
+            dst_ref=counts.at[2 * k + 1],
+            send_sem=count_send_sem.at[k],
+            recv_sem=count_recv_sem.at[k],
+            device_id=(partner(gx, 2**k, n_gx), gy),
+            device_id_type=MESH,
+        )
+
+    def count_join(k):
+        count_send(k).wait()
+        one, other = counts[2 * k], counts[2 * k + 1]
+        counts[2 * k + 2] = jnp.where(fill_here, jnp.maximum(one, other), one + other)
+
+    count_send(0).start()
 
     eye = lax.broadcasted_iota(jnp.int32, (slots, slots), 0) == lax.broadcasted_iota(jnp.int32, (slots, slots), 1)
     for m in range(members_dev):
@@ -764,7 +766,11 @@
     for buf in (sum_policy, sum_kl):
         per_member = [row_of(jnp.sum(buf[m], axis=1, keepdims=True)) for m in range(members_dev)]
         sums.append(row_sums(place, targets, per_member))
-    tails_send[...] = tiles(sums, jnp.broadcast_to(local_fill, (n_gy, 8, LANES)))
+    for k in range(1, rounds):
+        count_join(k - 1)
+        count_send(k).start()
+    count_join(rounds - 1)
+    tails_send[...] = tiles(sums, jnp.broadcast_to(counts[2 * rounds][None], (n_gy, 8, LANES)))
     tail_copies = tile_sends(tails_send, tails_recv, tail_send_sem, tail_recv_sem, range(1, n_gy))
     for copy in tail_copies:
         copy.start()
@@ -774,12 +780,7 @@
         copy.start()
 
 
-    for copy in count_copies:
-        copy.wait()
-    tokens = counts[0]
-    for off in range(1, n_gx):
-        tokens = tokens + counts[off]
-    ntok = tokens[:1, info_lane : info_lane + 1]
+    ntok = counts[2 * rounds][:1, info_lane : info_lane + 1]
     scale = samples * seq / ntok
     got_len = column_in(arrived, 0).reshape(total_rows, 1)
     got_row = row_of(got_len)
@@ -857,10 +858,6 @@
     for copy in tail_copies:
         copy.wait()
     ends = tails_recv[...]
-    needs[0] = jnp.max(ends, axis=0)
-    need_copies = axis_sends(needs, need_send_sem, need_recv_sem)
-    for copy in need_copies:
-        copy.start()
     first_sum = column_in(ends, 0).reshape(members, part, 1)
     second_sum = column_in(ends, 1).reshape(members, part, 1)
     value = (second_sum - advantage * first_sum) * (samples / ntok)[None]
@@ -868,12 +865,7 @@
     spread = lax.broadcasted_iota(jnp.int32, shape, 1) == lax.broadcasted_iota(jnp.int32, shape, 2)
     loss_ref[...] = jnp.sum(jnp.where(spread, value, 0.0), axis=1)[:, :part]
     adv_ref[...] = jnp.sum(jnp.where(spread, advantage, 0.0), axis=1)[:, :part]
-    for copy in need_copies:
-        copy.wait()
-    fullest = needs[0]
-    for off in range(1, n_gx):
-        fullest = jnp.maximum(fullest, needs[off])
-    over_ref[0, 0] = (jnp.max(fullest[:, fill_lane : fill_lane + 1]) > STRIP_BLOCKS).astype(jnp.int32)
+    over_ref[0, 0] = (jnp.max(ends[:, :, fill_lane : fill_lane + 1]) > STRIP_BLOCKS).astype(jnp.int32)
     for off in FIRST_ORDER:
         landed = heads_in.at[0]
         pltpu.make_async_copy(landed, landed, first_send_sem.at[off - 2]).wait()
@@ -1005,8 +997,7 @@
             pltpu.VMEM(tile, f32),
             pltpu.VMEM(tile, f32),
             pltpu.VMEM(tile, f32),
-            pltpu.VMEM((n_gx, 8, LANES), f32),
-            pltpu.VMEM((n_gx, 8, LANES), f32),
+            pltpu.VMEM((2 * n_gx, 8, LANES), f32),
             dma((3,)),
             dma((2, PIECES)),
             dma((2,)),
@@ -1021,10 +1012,8 @@
             dma((n_gy - 1,)),
             dma((n_gy - 1,)),
             dma((n_gy - 1,)),
-            dma((n_gx - 1,)),
-            dma((n_gx - 1,)),
-            dma((n_gx - 1,)),
-            dma((n_gx - 1,)),
+            dma((n_gx,)),
+            dma((n_gx,)),
         ],
         compiler_params=pltpu.CompilerParams(collective_id=0, has_side_effects=True, vmem_limit_bytes=36 * 2**20),
     )(policy_logp, anchor_logp, lengths, rewards, slot_prompt)
@@ -1056,7 +1045,7 @@
 def body(n_gx, n_gy, *args):
     members_dev, slots, seq = args[0].shape
     pool = 2 * members_dev * slots // n_gy
-    packs = n_gy == 8 and pool == ROLES * STRIPS and slots == LANES and seq == LANES * 32 and seq % (PIECES * LANES) == 0
+    packs = n_gy == 8 and n_gx in (2, 4, 8) and pool == ROLES * STRIPS and slots == LANES and seq == LANES * 32 and seq % (PIECES * LANES) == 0
     return (packed_body if packs else unpacked_body)(n_gx, n_gy, *args)
 
 

time: 43.4 us -> 42.3 us (0.975)
  Pallas kernels: 42.5 us -> 41.5 us
    pallas_call x1, Pallas kernels: 40.3 us -> 39.3 us  [packed_body(): pl.pallas_call(functools.partial(packed_exchange, n_gx, n_gy), out_shape=...]
where the time goes in v4:
time: 42.3 us; the launch traced here: 42.2 us
  Pallas kernels  41.5 us (98%)
  between operations  0.69 us (2%)
    pallas_call x1, Pallas kernels, packed_body(): pl.pallas_call(functools.partial(packed_exchange, n_gx, n_gy), out_shape=...  39.3 us
    pallas_call x1, Pallas kernels, fits(): pl.pallas_call(functools.partial(store, n_gy), out_shape=(jax.ShapeDtypeS...  2.16 us

profile of v4, /device:TPU:0, one launch (start us, length us, event | category | flops | bytes accessed | tf_op | source)
XLA Modules:
  0.0 42.2 jit_solution(14039591133688244650)
XLA Ops:
  0.6 0.0 copy-start
  0.6 0.0 copy-start.1
  0.7 0.0 copy-start.2
  0.7 39.3 %shard_map.82 = (f32[16,16,4096]{2,1,0:T(8,128)S(1)}, f32[16,16]{1,0:T(8,128)S(1)}, f32[16,16]{1,0:T(8,128)S(1)}, s32[1,1]{1,0:T(1,128)S(4)}, f32[4,2,8,8448]{3,...) custom-call(f32[2,128,4096]{2,1,0:T(8,128)} %policy_hbm.1, ...), custom_call_target="tpu_custom_call" | custom-call | tf_op jit(solution)/shard_map/pallas_call | solution.py:967
  40.0 0.0 copy-done
  40.0 0.0 copy-done.1
  40.0 0.0 copy-done.2
  40.0 2.2 %conditional.1 = ((f32[16,16,4096]{2,1,0:T(8,128)}, f32[16,16]{1,0:T(8,128)}, f32[16,16]{1,0:T(8,128)})) conditional(s32[]{:T(128)} %bitcast, (f32[16,16,4096]{2,1,0:T(8,128)S(1)}, f32[16,16]{1,0:T(8,128)S(1)}, f32[16,16]{1,0:T(8,128)S(1)}, f32[4,2,8,8448]{3,2,1,0:T(8,128)S(1)}, bf16[4,2,64,128]{3,2,1,0:T(8,128)(2,1)S(1)}, ...), branch_computations={%region_0.0_spmd, %region_1.0_spmd} | conditional | bytes 8 | solution.py:1039
  40.0 2.2 %branch_0_fun.1 = (f32[16,16,4096]{2,1,0:T(8,128)}, f32[16,16]{1,0:T(8,128)}, f32[16,16]{1,0:T(8,128)}) custom-call(f32[16,16,4096]{2,1,0:T(8,128)S(1)} %get-tuple-element.30.done, f32[16,16]{1,0:T(8,128)S(1)} %get-tuple-element.31.loss, f32[16,16]{1,0:T(8,128)S(1)} %get-tuple-element.32.adv, f32[4,2,8,8448]{3,2,1,0:T(8,128)S(1)} %get-tuple-element.33.recvbuf, ...), custom_call_target="tpu_custom_call" | custom-call | tf_op jit(solution)/shard_map/cond/branch_0_fun/pallas_call | solution.py:1023
Async XLA Ops:
  0.6 39.4 %copy-start = (s32[2,128]{1,0:T(2,128)S(1)}, s32[2,128]{1,0:T(2,128)}, u32[]{:S(2)}) copy-start(s32[2,128]{1,0:T(2,128)} %len_hbm.1) | copy-start | bytes 3076
  0.6 39.4 %copy-start.1 = (s32[2,128]{1,0:T(2,128)S(1)}, s32[2,128]{1,0:T(2,128)}, u32[]{:S(2)}) copy-start(s32[2,128]{1,0:T(2,128)} %reward_hbm.1) | copy-start | bytes 3076
  0.7 39.4 %copy-start.2 = (s32[2,128]{1,0:T(2,128)S(1)}, s32[2,128]{1,0:T(2,128)}, u32[]{:S(2)}) copy-start(s32[2,128]{1,0:T(2,128)} %prompt_hbm.1) | copy-start | bytes 3076

commit v5 on v4

--- a/solution.py
+++ b/solution.py
@@ -451,7 +451,7 @@
     total_rows = chips * pool
     samples = members * slots * n_gx
     info_lane, fill_lane = 16, 17
-    rounds = n_gx.bit_length() - 1
+    inner = (gx == 1) | (gx == 2)
     f32 = jnp.float32
 
     small_loads = [
@@ -473,8 +473,12 @@
     barrier = pltpu.get_barrier_semaphore()
     for off in range(1, n_gy):
         pl.semaphore_signal(barrier, inc=1, device_id=(gx, partner(gy, off, n_gy)), device_id_type=MESH)
-    for k in range(rounds):
-        pl.semaphore_signal(barrier, inc=1, device_id=(partner(gx, 2**k, n_gx), gy), device_id_type=MESH)
+    pl.semaphore_signal(barrier, inc=1, device_id=(partner(gx, 1, n_gx), gy), device_id_type=MESH)
+
+    @pl.when(inner)
+    def _():
+        pl.semaphore_signal(barrier, inc=1, device_id=(n_gx - 1 - gx, gy), device_id_type=MESH)
+
     for c in range(1, PIECES):
         for copy in loads(c):
             copy.start()
@@ -581,7 +585,7 @@
 
         @pl.when(c == 0)
         def _():
-            pl.semaphore_wait(barrier, n_gy - 1 + rounds)
+            pl.semaphore_wait(barrier, n_gy + lax.rem((gx + 1) // 2, 2))
             for off in FIRST_ORDER:
                 first_send(off, 0, piece).start()
             lens_out = row_sums(place, targets, lens)
@@ -727,22 +731,23 @@
     fill_here = lax.broadcasted_iota(jnp.int32, (8, LANES), 1) == fill_lane
     counts[0] = jnp.where(fill_here, local_fill, jnp.sum(arrived, axis=0))
 
-    def count_send(k):
+    def count_send(k, to):
         return pltpu.make_async_remote_copy(
             src_ref=counts.at[2 * k],
             dst_ref=counts.at[2 * k + 1],
             send_sem=count_send_sem.at[k],
             recv_sem=count_recv_sem.at[k],
-            device_id=(partner(gx, 2**k, n_gx), gy),
+            device_id=(to, gy),
             device_id_type=MESH,
         )
 
+    pair, across = partner(gx, 1, n_gx), n_gx - 1 - gx
+
     def count_join(k):
-        count_send(k).wait()
         one, other = counts[2 * k], counts[2 * k + 1]
-        counts[2 * k + 2] = jnp.where(fill_here, jnp.maximum(one, other), one + other)
-
-    count_send(0).start()
+        return jnp.where(fill_here, jnp.maximum(one, other), one + other)
+
+    count_send(0, pair).start()
 
     eye = lax.broadcasted_iota(jnp.int32, (slots, slots), 0) == lax.broadcasted_iota(jnp.int32, (slots, slots), 1)
     for m in range(members_dev):
@@ -766,11 +771,24 @@
     for buf in (sum_policy, sum_kl):
         per_member = [row_of(jnp.sum(buf[m], axis=1, keepdims=True)) for m in range(members_dev)]
         sums.append(row_sums(place, targets, per_member))
-    for k in range(1, rounds):
-        count_join(k - 1)
-        count_send(k).start()
-    count_join(rounds - 1)
-    tails_send[...] = tiles(sums, jnp.broadcast_to(counts[2 * rounds][None], (n_gy, 8, LANES)))
+    count_send(0, pair).wait()
+    counts[2] = count_join(0)
+
+    @pl.when(inner)
+    def _():
+        count_send(1, across).start()
+        count_send(1, across).wait()
+        counts[4] = count_join(1)
+        count_send(2, pair).start()
+        count_send(2, pair).wait_send()
+        counts[6] = counts[4]
+
+    @pl.when(jnp.logical_not(inner))
+    def _():
+        count_send(2, pair).wait_recv()
+        counts[6] = counts[5]
+
+    tails_send[...] = tiles(sums, jnp.broadcast_to(counts[6][None], (n_gy, 8, LANES)))
     tail_copies = tile_sends(tails_send, tails_recv, tail_send_sem, tail_recv_sem, range(1, n_gy))
     for copy in tail_copies:
         copy.start()
@@ -780,7 +798,7 @@
         copy.start()
 
 
-    ntok = counts[2 * rounds][:1, info_lane : info_lane + 1]
+    ntok = counts[6][:1, info_lane : info_lane + 1]
     scale = samples * seq / ntok
     got_len = column_in(arrived, 0).reshape(total_rows, 1)
     got_row = row_of(got_len)
@@ -1045,7 +1063,7 @@
 def body(n_gx, n_gy, *args):
     members_dev, slots, seq = args[0].shape
     pool = 2 * members_dev * slots // n_gy
-    packs = n_gy == 8 and n_gx in (2, 4, 8) and pool == ROLES * STRIPS and slots == LANES and seq == LANES * 32 and seq % (PIECES * LANES) == 0
+    packs = n_gy == 8 and n_gx == 4 and pool == ROLES * STRIPS and slots == LANES and seq == LANES * 32 and seq % (PIECES * LANES) == 0
     return (packed_body if packs else unpacked_body)(n_gx, n_gy, *args)
 
 

time: 42.3 us -> 41.7 us (0.986)
  Pallas kernels: 41.5 us -> 40.8 us
    pallas_call x1, Pallas kernels: 39.3 us -> 38.7 us  [packed_body(): pl.pallas_call(functools.partial(packed_exchange, n_gx, n_gy), out_shape=...]
where the time goes in v5:
time: 41.7 us; the launch traced here: 41.5 us
  Pallas kernels  40.8 us (98%)
  between operations  0.69 us (2%)
    pallas_call x1, Pallas kernels, packed_body(): pl.pallas_call(functools.partial(packed_exchange, n_gx, n_gy), out_shape=...  38.7 us
    pallas_call x1, Pallas kernels, fits(): pl.pallas_call(functools.partial(store, n_gy), out_shape=(jax.ShapeDtypeS...  2.15 us

profile of v5, /device:TPU:0, one launch (start us, length us, event | category | flops | bytes accessed | tf_op | source)
XLA Modules:
  0.0 41.5 jit_solution(1461526395568282430)
XLA Ops:
  0.6 0.0 copy-start
  0.6 0.0 copy-start.1
  0.7 0.0 copy-start.2
  0.7 38.7 %shard_map.82 = (f32[16,16,4096]{2,1,0:T(8,128)S(1)}, f32[16,16]{1,0:T(8,128)S(1)}, f32[16,16]{1,0:T(8,128)S(1)}, s32[1,1]{1,0:T(1,128)S(4)}, f32[4,2,8,8448]{3,...) custom-call(f32[2,128,4096]{2,1,0:T(8,128)} %policy_hbm.1, ...), custom_call_target="tpu_custom_call" | custom-call | tf_op jit(solution)/shard_map/pallas_call | solution.py:985
  39.3 0.0 copy-done
  39.3 0.0 copy-done.1
  39.3 0.0 copy-done.2
  39.4 2.2 %conditional.1 = ((f32[16,16,4096]{2,1,0:T(8,128)}, f32[16,16]{1,0:T(8,128)}, f32[16,16]{1,0:T(8,128)})) conditional(s32[]{:T(128)} %bitcast, (f32[16,16,4096]{2,1,0:T(8,128)S(1)}, f32[16,16]{1,0:T(8,128)S(1)}, f32[16,16]{1,0:T(8,128)S(1)}, f32[4,2,8,8448]{3,2,1,0:T(8,128)S(1)}, bf16[4,2,64,128]{3,2,1,0:T(8,128)(2,1)S(1)}, ...), branch_computations={%region_0.0_spmd, %region_1.0_spmd} | conditional | bytes 8 | solution.py:1057
  39.4 2.1 %branch_0_fun.1 = (f32[16,16,4096]{2,1,0:T(8,128)}, f32[16,16]{1,0:T(8,128)}, f32[16,16]{1,0:T(8,128)}) custom-call(f32[16,16,4096]{2,1,0:T(8,128)S(1)} %get-tuple-element.30.done, f32[16,16]{1,0:T(8,128)S(1)} %get-tuple-element.31.loss, f32[16,16]{1,0:T(8,128)S(1)} %get-tuple-element.32.adv, f32[4,2,8,8448]{3,2,1,0:T(8,128)S(1)} %get-tuple-element.33.recvbuf, ...), custom_call_target="tpu_custom_call" | custom-call | tf_op jit(solution)/shard_map/cond/branch_0_fun/pallas_call | solution.py:1041
Async XLA Ops:
  0.6 38.7 %copy-start = (s32[2,128]{1,0:T(2,128)S(1)}, s32[2,128]{1,0:T(2,128)}, u32[]{:S(2)}) copy-start(s32[2,128]{1,0:T(2,128)} %len_hbm.1) | copy-start | bytes 3076
  0.6 38.7 %copy-start.1 = (s32[2,128]{1,0:T(2,128)S(1)}, s32[2,128]{1,0:T(2,128)}, u32[]{:S(2)}) copy-start(s32[2,128]{1,0:T(2,128)} %reward_hbm.1) | copy-start | bytes 3076
  0.7 38.7 %copy-start.2 = (s32[2,128]{1,0:T(2,128)S(1)}, s32[2,128]{1,0:T(2,128)}, u32[]{:S(2)}) copy-start(s32[2,128]{1,0:T(2,128)} %prompt_hbm.1) | copy-start | bytes 3076
